TPU v7x, 256 devices: a whole 4x4x8 slice. The times are simulated.
256 devices in a mesh: rows: 32 (over x, y, core), feat: 8 (over z).
Axes of the slice: x: 4, y: 4, z: 8, core: 2. Of those that a mesh axis runs over, the one named last changes fastest.
Arguments:
- queries: bfloat16 [196608, 4096], P('rows', 'feat'), may hold values from -6 to 6
- projection: bfloat16 [4096, 128], P('feat'), may hold values from -0.09375 to 0.09375
- models: float32 [64, 128], replicated, may hold values from -0.5 to 0.5
- first: int32 [196608], P('rows'), may hold values from 0 to 63
- second: int32 [196608], P('rows'), may hold values from 0 to 63
- wins: int32 [196608], P('rows'), may hold values 0 or 1
Outputs:
- update_proj: float32 [4096, 128], P('feat')
- update_models: float32 [64, 128], replicated
- loss: float32 [], replicated
All inputs are finite; a program needn't handle non-finite values. No bound on the sum of `wins` on one device may be relied on, other than what follows from the above.
Results may differ from a plain program's by a relative error of at most 0.00045.
The roundings to bfloat16 on the way count: a program that leaves them out, or rounds other values in their place, can miss the bound.
Values may be sent and summed in bfloat16 or wider, within the bound.
No kernel may reach another device: no remote copies, remote signals or barrier semaphores. Data moves between devices by JAX's collectives and lax.ppermute only.
A program may use at most 64 MiB of HBM per device.

v0:
```python
import functools

import jax
import jax.numpy as jnp
from jax import lax
from jax.sharding import Mesh
from jax.sharding import PartitionSpec as P

D = 4096
R = 128
NM = 64
ROWS = ("rows_0", "rows_1", "rows_2")
ROWS_FEAT = ("rows_0", "rows_1", "rows_2", "feat")


def from_everyone(x, axis):
    copies = jnp.broadcast_to(x, (lax.axis_size(axis), *x.shape))
    return lax.all_to_all(copies, axis, split_axis=0, concat_axis=0, tiled=True)


def over_copies(x, axis):
    everything = from_everyone(x, axis)
    return jnp.sum(everything, axis=0)


def over_axes(x, axes):
    return functools.reduce(lax.psum, axes, x)


def cut_along(x, dim, count):
    lengths = x.shape
    parts = x.reshape(*lengths[:dim], count, lengths[dim] // count, *lengths[dim + 1 :])
    return jnp.moveaxis(parts, dim, 0)


def summed_on_arrival(x, axis, dim):
    count = lax.axis_size(axis)
    parts = lax.all_to_all(cut_along(x, dim, count), axis, 0, 0, tiled=True)
    return jnp.sum(parts, axis=0)


def in_order(parts, dim):
    parts = jnp.moveaxis(parts, 0, dim)
    lengths = parts.shape
    return parts.reshape(*lengths[:dim], lengths[dim] * lengths[dim + 1], *lengths[dim + 2 :])


def gathered_copies(x, axis, dim):
    return in_order(from_everyone(x, axis), dim)


def pair_gap(models, first, second):
    return jnp.take(models, first, axis=0) - jnp.take(models, second, axis=0)


def pick_table(models, first, second):
    labels = jnp.arange(models.shape[0], dtype=jnp.int32)[:, None]
    return (labels == first[None, :]).astype(jnp.float32) - (labels == second[None, :]).astype(
        jnp.float32
    )


def body(queries, projection, models, first, second, wins):
    local_rows = queries.shape[0]
    total_rows = float(local_rows * lax.axis_size(ROWS))
    partial_value = jnp.dot(queries, projection, preferred_element_type=jnp.float32)
    gap = pair_gap(models, first, second)
    margin = over_copies(jnp.sum(partial_value * gap, axis=-1), "feat")
    sign = 2.0 * wins.astype(jnp.float32) - 1.0
    loss_part = jnp.sum(jax.nn.softplus(-sign * margin)) / total_rows
    coef = -sign * jax.nn.sigmoid(-sign * margin) / total_rows
    back = (coef[:, None] * gap).astype(jnp.bfloat16)
    pick = pick_table(models, first, second)
    model_part = jnp.dot(pick, coef[:, None] * partial_value, precision=lax.Precision.HIGHEST)
    feat_count = float(lax.axis_size("feat"))
    grad_models, loss = (
        over_axes(model_part, ROWS_FEAT),
        over_axes(loss_part / feat_count, ROWS_FEAT),
    )
    model_square = jnp.sum(grad_models * grad_models)
    entries = jnp.sqrt(jnp.float32(D * R + NM * R))
    grad_share = summed_on_arrival(
        lax.dot_general(
            queries, back, (((0,), (0,)), ((), ())), preferred_element_type=jnp.float32
        ),
        ROWS,
        0,
    )
    square = over_axes(jnp.sum(grad_share * grad_share), ROWS_FEAT)
    scale = entries / (jnp.sqrt(square + model_square) + 1e-06)
    update_proj = gathered_copies(scale * grad_share, ROWS, 0)
    return (update_proj, scale * grad_models, loss)


def solution(mesh):
    split = Mesh(
        mesh.devices.reshape(4, 4, 2, mesh.shape["feat"]), ("rows_0", "rows_1", "rows_2", "feat")
    )
    in_specs = (P(ROWS, "feat"), P("feat", None), P(), P(ROWS), P(ROWS), P(ROWS))
    out_specs = (P("feat", None), P(), P())
    return jax.shard_map(body, mesh=split, in_specs=in_specs, out_specs=out_specs, check_vma=False)
```

profile of v0, /device:TPU:1, one launch (start us, length us, event | category | flops | bytes accessed | tf_op | source)
XLA Modules:
  0.0 185.9 jit_solution(2346574674489730573)
XLA Ops:
  0.7 0.8 fusion.13
  1.4 0.8 compare_and_fusion
  2.2 0.7 fusion.14
  3.0 20.9 %gather_fusion.1 = f32[6144,128]{1,0:T(8,128)} fusion(f32[64,128]{1,0:T(8,128)S(1)} %copy-done.1, s32[6144]{0:T(1024)S(1)} %fusion.14), kind=kCustom, calls=%fused_computation.1.clone | custom fusion | bytes 6316032 | tf_op jit(solution)/shard_map/jit(_take)/gather | solution.py:53
  23.9 2.4 %copy.18 = f32[6144,128]{0,1:T(8,128)S(1)} copy(f32[6144,128]{1,0:T(8,128)} %gather_fusion.1) | data formatting | bytes 6291456 | tf_op jit(solution)/shard_map/jit(_take)/gather | solution.py:53
  26.3 20.9 %gather_fusion = f32[6144,128]{1,0:T(8,128)} fusion(f32[64,128]{1,0:T(8,128)S(1)} %copy-done.1, s32[6144]{0:T(1024)S(1)} %fusion.13), kind=kCustom, calls=%fused_computation.clone | custom fusion | bytes 6316032 | tf_op jit(solution)/shard_map/jit(_take)/gather | solution.py:53
  47.1 3.5 %copy.17 = f32[6144,128]{0,1:T(8,128)} copy(f32[6144,128]{1,0:T(8,128)} %gather_fusion) | data formatting | bytes 6291456 | tf_op jit(solution)/shard_map/jit(_take)/gather | solution.py:53
  50.7 7.6 %multiply_reduce_fusion = (f32[6144]{0:T(1024)S(1)}, f32[6144,128]{0,1:T(8,128)}) fusion(f32[6144,128]{0,1:T(8,128)S(1)} %copy.18, pred[6144]{0:T(1024)(128)(4,1)S(1)} %get-tuple-element.20, f32[6144,128]{0,1:T(8,128)} %copy.17, pred[6144]{0:T(1024)(128)(4,1)S(1)} %get-tuple-element.21, bf16[6144,512]{1,0:T(8,128)(2,1)} %param.8, ...), kind=kOutput, calls=%fused_computation.6 | convolution fusion | flops 809232384 | bytes 15896576 | tf_op jit(solution)/shard_map/dot_general | solution.py:66
  58.4 17.8 %all_to_all.16 = f32[8,1,6144]{2,1,0:T(1,128)S(1)} all-to-all(f32[8,1,6144]{2,1,0:T(1,128)S(1)} %broadcast_in_dim.20), channel_id=1, replica_groups=mesh['rows_0'=4,'rows_1'=4,'rows_2'=2,'feat'=8] {'feat'}, dimensions={0} | all-to-all | bytes 393216 | tf_op jit(solution)/shard_map/all_to_all | solution.py:18
  76.4 0.6 fusion.11
  77.6 4.7 %fusion.8 = f32[512,128]{0,1:T(8,128)S(1)} fusion(bf16[6144,512]{1,0:T(8,128)(2,1)} %param.8, f32[6144]{0:T(1024)S(1)} %get-tuple-element.17, f32[6144,128]{0,1:T(8,128)S(1)} %copy.18, f32[6144,128]{0,1:T(8,128)} %copy.17, pred[6144]{0:T(1024)(128)(4,1)S(1)} %get-tuple-element.20, pred[6144]{0:T(1024)(128)(4,1)S(1)} %get-tuple-element.21), kind=kOutput, calls=%fused_computation.15 | convolution fusion | flops 809238528 | bytes 12881920 | tf_op jit(solution)/shard_map/dot_general | solution.py:83
  82.3 0.8 copy.20
  83.2 9.5 %all-to-all-start.1 = ((f32[32,16,128]{2,1,0:T(8,128)}), f32[32,16,128]{2,1,0:T(8,128)S(1)}, u32[]{:S(2)}, u32[]{:S(2)}) async-start(f32[32,16,128]{2,1,0:T(8,128)} %bitcast.1), calls=%async_computation.1 | async-start | bytes 524288 | tf_op jit(solution)/shard_map/all_to_all | solution.py:38
  93.3 5.2 %fusion = f32[64,128]{1,0:T(8,128)S(1)} fusion(f32[6144,128]{0,1:T(8,128)} %get-tuple-element.19, f32[6144]{0:T(1024)} %copy-done.2, s32[6144]{0:T(1024)} %param.12, s32[6144]{0:T(1024)} %param.11), kind=kOutput, calls=%fused_computation.3 | convolution fusion | flops 606732288 | bytes 3252224 | tf_op jit(solution)/shard_map/dot_general | solution.py:74
  98.6 3.1 %all-to-all-done.1 = f32[32,16,128]{2,1,0:T(8,128)S(1)} async-done(((f32[32,16,128]{2,1,0:T(8,128)}), f32[32,16,128]{2,1,0:T(8,128)S(1)}, u32[]{:S(2)}, u32[]{:S(2)}) %all-to-all-start.1) | async-done | bytes 262176 | tf_op jit(solution)/shard_map/all_to_all | solution.py:38
  102.3 12.9 %all-reduce.2 = (f32[]{:T(128)}, f32[64,128]{1,0:T(8,128)S(1)}, f32[]{:T(128)}) all-reduce(f32[]{:T(128)} %multiply_reduce_fusion.2, f32[64,128]{1,0:T(8,128)S(1)} %fusion, f32[]{:T(128)S(6)} %div.20), channel_id=1, replica_groups=mesh['rows_0'=4,'rows_1'=4,'rows_2'=2,'feat'=8] {'rows_0'}, use_global_device_ids=true, to_apply=%region_4.6 | all-reduce | flops 8194 | bytes 65552 | tf_op jit(solution)/shard_map/psum | solution.py:27
  115.2 13.3 %all-reduce.1 = (f32[]{:T(128)}, f32[64,128]{1,0:T(8,128)S(1)}, f32[]{:T(128)}) all-reduce(f32[]{:T(128)} %get-tuple-element.10, f32[64,128]{1,0:T(8,128)S(1)} %get-tuple-element.11, f32[]{:T(128)} %get-tuple-element.12), channel_id=1, replica_groups=mesh['rows_0'=4,'rows_1'=4,'rows_2'=2,'feat'=8] {'rows_1'}, use_global_device_ids=true, to_apply=%region_5.7 | all-reduce | flops 8194 | bytes 65552 | tf_op jit(solution)/shard_map/psum | solution.py:27
  128.5 12.2 %all-reduce.3 = (f32[]{:T(128)}, f32[64,128]{1,0:T(8,128)S(1)}, f32[]{:T(128)}) all-reduce(f32[]{:T(128)} %get-tuple-element.7, f32[64,128]{1,0:T(8,128)S(1)} %get-tuple-element.8, f32[]{:T(128)} %get-tuple-element.9), channel_id=1, replica_groups=mesh['rows_0'=4,'rows_1'=4,'rows_2'=2,'feat'=8] {'rows_2'}, use_global_device_ids=true, to_apply=%region_6.8 | all-reduce | flops 8194 | bytes 65552 | tf_op jit(solution)/shard_map/psum | solution.py:27
  140.7 21.7 %all-reduce = (f32[]{:T(128)}, f32[64,128]{1,0:T(8,128)S(1)}, f32[]{:T(128)}) all-reduce(f32[]{:T(128)} %get-tuple-element.13, f32[64,128]{1,0:T(8,128)S(1)} %get-tuple-element.14, f32[]{:T(128)} %get-tuple-element.15), channel_id=1, replica_groups=mesh['rows_0'=4,'rows_1'=4,'rows_2'=2,'feat'=8] {'feat'}, use_global_device_ids=true, to_apply=%region_7.9 | all-reduce | flops 8194 | bytes 65552 | tf_op jit(solution)/shard_map/psum | solution.py:27
  164.4 0.7 broadcast_in_dim.21
  165.2 10.9 %all-to-all-start.2 = ((f32[32,16,128]{2,1,0:T(8,128)}), f32[32,16,128]{2,1,0:T(8,128)S(1)}, u32[]{:S(2)}, u32[]{:S(2)}) async-start(f32[32,16,128]{2,1,0:T(8,128)} %broadcast_in_dim.21), calls=%async_computation.2 | async-start | bytes 524288 | tf_op jit(solution)/shard_map/all_to_all | solution.py:18
  176.1 0.6 broadcast_multiply_fusion
  176.7 8.4 %all-to-all-done.2 = f32[32,16,128]{2,1,0:T(8,128)S(1)} async-done(((f32[32,16,128]{2,1,0:T(8,128)}), f32[32,16,128]{2,1,0:T(8,128)S(1)}, u32[]{:S(2)}, u32[]{:S(2)}) %all-to-all-start.2) | async-done | bytes 262176 | tf_op jit(solution)/shard_map/all_to_all | solution.py:18
  185.2 0.7 copy.23
  (14 shorter events, 2.1 us)
Async XLA Ops:
  0.6 50.0 %copy-start = (bf16[512,128]{1,0:T(8,128)(2,1)S(1)}, bf16[512,128]{1,0:T(8,128)(2,1)}, u32[]{:S(2)}) copy-start(bf16[512,128]{1,0:T(8,128)(2,1)} %param.9) | copy-start | bytes 393220
  0.6 2.3 %copy-start.1 = (f32[64,128]{1,0:T(8,128)S(1)}, f32[64,128]{1,0:T(8,128)}, u32[]{:S(2)}) copy-start(f32[64,128]{1,0:T(8,128)} %param.10) | copy-start | bytes 98308
  50.7 25.7 %copy-start.3 = (s32[6144]{0:T(1024)S(1)}, s32[6144]{0:T(1024)}, u32[]{:S(2)}) copy-start(s32[6144]{0:T(1024)} %param.13) | copy-start | bytes 73732
  77.0 0.6 copy-start.2
  83.2 18.5 %all-to-all-start.1 = ((f32[32,16,128]{2,1,0:T(8,128)}), f32[32,16,128]{2,1,0:T(8,128)S(1)}, u32[]{:S(2)}, u32[]{:S(2)}) async-start(f32[32,16,128]{2,1,0:T(8,128)} %bitcast.1), calls=%async_computation.1 | async-start | bytes 524288 | tf_op jit(solution)/shard_map/all_to_all | solution.py:38
  165.2 20.0 %all-to-all-start.2 = ((f32[32,16,128]{2,1,0:T(8,128)}), f32[32,16,128]{2,1,0:T(8,128)S(1)}, u32[]{:S(2)}, u32[]{:S(2)}) async-start(f32[32,16,128]{2,1,0:T(8,128)} %broadcast_in_dim.21), calls=%async_computation.2 | async-start | bytes 524288 | tf_op jit(solution)/shard_map/all_to_all | solution.py:18
where the time goes:
time: 186 us
  blocking collectives  77.9 us (42%)
  local copies, waits for them, and re-layouts  50.6 us (27%)
  starting transfers between devices  20.5 us (11%)
  matrix products  17.6 us (9%)
  waiting for transfers between devices  11.5 us (6%)
  other arithmetic  4.96 us (3%)
  between operations  2.76 us (1%)
    psum x4, blocking collectives, over_axes(): return functools.reduce(lax.psum, axes, x)  60.1 us
    gather x4, local copies, waits for them, and re-layouts, pair_gap(): return jnp.take(models, first, axis=0) - jnp.take(models, second, axis=0)  47.7 us
    all_to_all x1, blocking collectives, from_everyone(): return lax.all_to_all(copies, axis, split_axis=0, concat_axis=0, tiled=True)  17.8 us
    all_to_all x1, starting transfers between devices, from_everyone(): return lax.all_to_all(copies, axis, split_axis=0, concat_axis=0, tiled=True)  10.9 us
    all_to_all x1, starting transfers between devices, summed_on_arrival(): parts = lax.all_to_all(cut_along(x, dim, count), axis, 0, 0, tiled=True)  9.52 us
    all_to_all x1, waiting for transfers between devices, from_everyone(): return lax.all_to_all(copies, axis, split_axis=0, concat_axis=0, tiled=True)  8.45 us
    dot_general x1, matrix products, body(): jnp.dot(queries, projection, preferred_element_type=jnp.float32)  7.64 us
    dot_general x1, matrix products, body(): jnp.dot(pick, coef[:, None] * partial_value, precision=lax.Precision.HIGH...  5.22 us
  transfers between devices with their start and end apart: 2, of which 2 were waited for; matrix products, arithmetic and copies ran while one was open for 3% of the time, Pallas kernels for 0%

commit v1 on v0

v1 whole, which is shorter than its diff:
```python
import functools

import jax
import jax.numpy as jnp
from jax import lax
from jax.experimental import pallas as pl
from jax.experimental.pallas import tpu as pltpu
from jax.sharding import Mesh
from jax.sharding import PartitionSpec as P

D = 4096
R = 128
NM = 64
LANES = 128
ROWS = ("rows_0", "rows_1", "rows_2")
F32 = jnp.float32
BF16 = jnp.bfloat16
MIB = 1 << 20
CHUNK = 1024


def exchange(x, axis):
    return lax.all_to_all(x, axis, split_axis=0, concat_axis=0, tiled=True)


def pieces(x, count):
    terms = []
    for _ in range(count):
        term = x.astype(BF16)
        terms.append(term)
        x = x - term.astype(F32)
    return terms


def contract(a, b, dim_a, dim_b):
    return lax.dot_general(a, b, (((dim_a,), (dim_b,)), ((), ())), preferred_element_type=F32)


def model_table(models):
    stacked = jnp.concatenate([term.astype(F32) for term in pieces(models, 3)], axis=0)
    return stacked.T.astype(BF16)


def picks(first_ref, second_ref, start, count):
    labels = lax.broadcasted_iota(jnp.int32, (NM, LANES), 0)
    tiles = []
    for i in range(start // LANES, (start + count) // LANES):
        one = jnp.where(labels == first_ref[i : i + 1, :], 1.0, 0.0)
        two = jnp.where(labels == second_ref[i : i + 1, :], 1.0, 0.0)
        tiles.append(one - two)
    return jnp.concatenate(tiles, axis=1)


def gaps(table, pick):
    pick = pick.astype(BF16)
    return contract(table, jnp.concatenate([pick, pick, pick], axis=0), 1, 0)


def margin_kernel(first_ref, second_ref, models_ref, proj_ref, q_hbm, out_ref, q_ref, sems):
    tokens = q_hbm.shape[0]
    copies = []
    for i in range(tokens // CHUNK):
        rows = pl.ds(i * CHUNK, CHUNK)
        copies.append(pltpu.make_async_copy(q_hbm.at[rows, :], q_ref.at[rows, :], sems.at[i]))
        copies[-1].start()
    table = model_table(models_ref[...])
    proj = proj_ref[...].astype(F32).T.astype(BF16)
    for i in range(tokens // CHUNK):
        gap = gaps(table, picks(first_ref, second_ref, i * CHUNK, CHUNK))
        copies[i].wait()
        routed = contract(proj, q_ref[pl.ds(i * CHUNK, CHUNK), :], 1, 1)
        margin = jnp.sum(routed * gap, axis=0, keepdims=True)
        for j in range(CHUNK // LANES):
            row = margin[:, j * LANES : (j + 1) * LANES]
            for k in range(out_ref.shape[0]):
                out_ref[k, pl.ds(i * (CHUNK // LANES) + j, 1), :] = row


def grad_kernel(total, share, margins_ref, first_ref, second_ref, wins_ref, models_ref, proj_ref, q_ref, out_ref, loss_ref, coef_ref, acc_ref):
    tokens = q_ref.shape[0]
    margin = margins_ref[0]
    for k in range(1, margins_ref.shape[0]):
        margin = margin + margins_ref[k]
    sign = 2.0 * wins_ref[...].astype(F32) - 1.0
    wrong = -sign * margin
    loss_ref[...] = jax.nn.softplus(wrong) / total
    coef_ref[...] = -sign * jax.nn.sigmoid(wrong) / total
    table = model_table(models_ref[...])
    for i in range(tokens // CHUNK):
        pick = picks(first_ref, second_ref, i * CHUNK, CHUNK)
        gap = gaps(table, pick)
        first_row = i * CHUNK // LANES
        coef = jnp.concatenate([coef_ref[first_row + j : first_row + j + 1, :] for j in range(CHUNK // LANES)], axis=1)
        left = jnp.concatenate([(coef * gap).astype(BF16), *pieces(coef * pick, 2)], axis=0)
        part = contract(left, q_ref[pl.ds(i * CHUNK, CHUNK), :], 1, 0)
        if i == 0:
            acc_ref[...] = part
        else:
            acc_ref[...] += part
    grad = acc_ref[:R, :].T
    weighted = acc_ref[R : R + NM, :] + acc_ref[R + NM :, :]
    model_terms = contract(jnp.concatenate(pieces(weighted, 3), axis=0), proj_ref[...], 1, 0)
    model_grad = model_terms[:NM] + model_terms[NM : 2 * NM] + model_terms[2 * NM :]
    count = out_ref.shape[0]
    for j in range(count):
        for i in range(share // 2):
            at = j * share + 2 * i
            out_ref[j, i] = grad[at : at + 2]
        for i in range(NM // count // 2):
            at = j * (NM // count) + 2 * i
            out_ref[j, share // 2 + i] = model_grad[at : at + 2]


def share_kernel(parts_ref, share_ref, out_ref):
    summed = parts_ref[0]
    for k in range(1, parts_ref.shape[0]):
        summed = summed + parts_ref[k]
    pairs = share_ref.shape[0]
    grad = summed[:pairs]
    share_ref[...] = grad
    square = jnp.sum(grad * grad, axis=0)
    for k in range(out_ref.shape[0]):
        out_ref[k, : summed.shape[0] - pairs] = summed[pairs:]
        out_ref[k, summed.shape[0] - pairs] = square


def pack_kernel(parts_ref, share_ref, loss_ref, out_ref):
    summed = parts_ref[0]
    for k in range(1, parts_ref.shape[0]):
        summed = summed + parts_ref[k]
    pairs = share_ref.shape[0]
    kinds = summed.shape[0] - 1
    model_grad = summed[:kinds]
    square = summed[kinds] + jnp.sum(model_grad * model_grad, axis=0)
    square = jnp.sum(square, axis=0, keepdims=True)
    loss = jnp.sum(loss_ref[...], axis=0, keepdims=True)
    grad = share_ref[...]
    for k in range(out_ref.shape[0]):
        out_ref[k, :pairs] = grad
        out_ref[k, pairs : pairs + kinds] = model_grad
        out_ref[k, pairs + kinds, 0:1] = square
        out_ref[k, pairs + kinds, 1:2] = loss


def final_kernel(share, parts_ref, proj_ref, models_ref, loss_ref):
    count, entries = parts_ref.shape[0], parts_ref.shape[1]
    pairs = share // 2
    kinds = entries - pairs - 1
    sums = parts_ref[0, entries - 1]
    for k in range(1, count):
        sums = sums + parts_ref[k, entries - 1]
    sums = jnp.sum(sums, axis=1, keepdims=True)
    loss_ref[...] = sums[1:2]
    scale = jnp.sqrt(F32(D * R + NM * R)) / (jnp.sqrt(sums[0:1]) + 1e-06)
    scale = jnp.broadcast_to(scale, (2, LANES))
    for k in range(count):
        for i in range(pairs):
            proj_ref[k * share + 2 * i : k * share + 2 * i + 2, :] = scale * parts_ref[k, i]
        for i in range(kinds):
            at = 2 * (k * kinds + i)
            models_ref[at : at + 2, :] = scale * parts_ref[k, pairs + i]


VMEM = pl.BlockSpec(memory_space=pltpu.VMEM)
HBM = pl.BlockSpec(memory_space=pltpu.HBM)


def kernel_call(body, outs, ins, name, limit, cost, in_specs=None, scratch=()):
    flops, moved = cost
    return pl.pallas_call(
        body,
        out_shape=outs,
        in_specs=in_specs or [VMEM] * len(ins),
        out_specs=jax.tree.map(lambda _: VMEM, outs),
        scratch_shapes=scratch,
        compiler_params=pltpu.CompilerParams(vmem_limit_bytes=limit * MIB),
        cost_estimate=pl.CostEstimate(flops=flops, bytes_accessed=moved, transcendentals=0),
        name=name,
    )(*ins)


def shape(*dims, kind=F32):
    return jax.ShapeDtypeStruct(dims, kind)


def body(queries, projection, models, first, second, wins):
    tokens, width = queries.shape
    rows, feats = lax.axis_size(ROWS), lax.axis_size("feat")
    share = width // rows
    kinds = NM // rows // 2
    first, second, wins = (x.reshape(tokens // LANES, LANES) for x in (first, second, wins))
    margins, held = kernel_call(
        margin_kernel,
        (shape(feats, tokens // LANES, LANES), pltpu.VMEM((tokens, width), BF16)),
        (first, second, models, projection, pltpu.with_memory_space_constraint(queries, pltpu.HBM)),
        "margins",
        24,
        (2 * tokens * width * R, tokens * width * 2),
        in_specs=[VMEM] * 4 + [HBM],
        scratch=[pltpu.SemaphoreType.DMA((tokens // CHUNK,))],
    )
    margins = exchange(margins, "feat")
    parts, loss = kernel_call(
        functools.partial(grad_kernel, float(tokens * rows), share),
        (shape(rows, share // 2 + kinds, 2, LANES), shape(tokens // LANES, LANES)),
        (margins, first, second, wins, models, projection, held),
        "grads",
        24,
        (4 * tokens * width * R, tokens * width * 2),
        scratch=[pltpu.VMEM((tokens // LANES, LANES), F32), pltpu.VMEM((R + 2 * NM, width), F32)],
    )
    parts = exchange(parts, ROWS)
    grad_share, parts = kernel_call(
        share_kernel,
        (shape(share // 2, 2, LANES), shape(feats, kinds + 1, 2, LANES)),
        (parts,),
        "shares",
        4,
        (10000, 400000),
    )
    parts = exchange(parts, "feat")
    parts = kernel_call(
        pack_kernel,
        shape(rows, share // 2 + kinds + 1, 2, LANES),
        (parts, grad_share, loss),
        "pack",
        4,
        (10000, 400000),
    )
    parts = exchange(parts, ROWS)
    update_proj, update_models, loss = kernel_call(
        functools.partial(final_kernel, share),
        (shape(width, R), shape(NM, R), shape(1, 1)),
        (parts,),
        "final",
        4,
        (10000, 600000),
    )
    return update_proj, update_models, loss.reshape(())


def solution(mesh):
    split = Mesh(
        mesh.devices.reshape(4, 4, 2, mesh.shape["feat"]), ("rows_0", "rows_1", "rows_2", "feat")
    )
    in_specs = (P(ROWS, "feat"), P("feat", None), P(), P(ROWS), P(ROWS), P(ROWS))
    out_specs = (P("feat", None), P(), P())
    return jax.shard_map(body, mesh=split, in_specs=in_specs, out_specs=out_specs, check_vma=False)
```

time: 186 us -> 72.5 us (0.39)
  local copies, waits for them, and re-layouts: 50.6 us -> 3.13 us
  starting transfers between devices: 20.5 us -> 0 us
  blocking collectives: 77.9 us -> 59.6 us
  matrix products: 17.6 us -> 0 us
  waiting for transfers between devices: 11.5 us -> 0 us
  Pallas kernels: 0 us -> 8.64 us
  other arithmetic: 4.96 us -> 0 us
  between operations: 2.76 us -> 0.67 us
    psum x4 -> x0, blocking collectives: 60.1 us -> none  [over_axes(): return functools.reduce(lax.psum, axes, x)]
    gather x4 -> x0, local copies, waits for them, and re-layouts: 47.7 us -> none  [pair_gap(): return jnp.take(models, first, axis=0) - jnp.take(models, second, axis=0)]
    all_to_all x1 -> x4, blocking collectives: 17.8 us -> 59.6 us  [exchange(): return lax.all_to_all(x, axis, split_axis=0, concat_axis=0, tiled=True)]
    all_to_all x2 -> x0, starting transfers between devices: 20.5 us -> none  [the longest x1 10.9 us: from_everyone(): return lax.all_to_all(copies, axis, split_axis=0, concat_axis=0, tiled=True)]
    dot_general x3 -> x0, matrix products: 17.6 us -> none  [the longest x1 7.64 us: body(): jnp.dot(queries, projection, preferred_element_type=jnp.float32)]
    all_to_all x2 -> x0, waiting for transfers between devices: 11.5 us -> none  [the longest x1 8.45 us: from_everyone(): return lax.all_to_all(copies, axis, split_axis=0, concat_axis=0, tiled=True)]
    pallas_call x0 -> x5, Pallas kernels: none -> 8.64 us  [kernel_call(): pl.pallas_call(body, out_shape=outs, in_specs=in_specs or [VMEM] * len(in...]
    reduce_sum x5 -> x0, other arithmetic: 2.02 us -> none  [the longest x1 0.63 us: body(): loss_part = jnp.sum(jax.nn.softplus(-sign * margin)) / total_rows]
  transfers between devices with their start and end apart: 2 -> 0, of which waited for: 2 -> 0; matrix products, arithmetic and copies ran while one was open for 3% -> 0% of each run, Pallas kernels for 0% -> 0%
where the time goes in v1:
time: 72.5 us; the launch traced here: 72 us
  blocking collectives  59.6 us (82%)
  Pallas kernels  8.64 us (12%)
  local copies, waits for them, and re-layouts  3.13 us (4%)
    all_to_all x4, blocking collectives, exchange(): return lax.all_to_all(x, axis, split_axis=0, concat_axis=0, tiled=True)  59.6 us
    pallas_call x5, Pallas kernels, kernel_call(): pl.pallas_call(body, out_shape=outs, in_specs=in_specs or [VMEM] * len(in...  8.64 us
    unnamed x10, local copies, waits for them, and re-layouts  3.13 us

profile of v1, /device:TPU:1, one launch (start us, length us, event | category | flops | bytes accessed | tf_op | source)
XLA Modules:
  0.0 72.0 jit_solution(7507204840930347185)
XLA Ops:
  0.6 0.0 copy-start
  0.6 0.9 %copy-done = bf16[512,128]{1,0:T(8,128)(2,1)S(1)} copy-done((bf16[512,128]{1,0:T(8,128)(2,1)S(1)}, bf16[512,128]{1,0:T(8,128)(2,1)}, u32[]{:S(2)}) %copy-start) | copy-done | bytes 131096
  1.5 0.0 copy-start.1
  1.5 0.8 %copy-done.1 = f32[64,128]{1,0:T(8,128)S(1)} copy-done((f32[64,128]{1,0:T(8,128)S(1)}, f32[64,128]{1,0:T(8,128)}, u32[]{:S(2)}) %copy-start.1) | copy-done | bytes 32792
  2.3 0.0 copy-start.2
  2.3 0.7 %copy-done.2 = s32[6144]{0:T(1024)S(1)} copy-done((s32[6144]{0:T(1024)S(1)}, s32[6144]{0:T(1024)}, u32[]{:S(2)}) %copy-start.2) | copy-done | bytes 24600
  3.0 0.0 copy-start.3
  3.0 0.7 %copy-done.3 = s32[6144]{0:T(1024)S(1)} copy-done((s32[6144]{0:T(1024)S(1)}, s32[6144]{0:T(1024)}, u32[]{:S(2)}) %copy-start.3) | copy-done | bytes 24600
  3.8 0.0 copy-start.4
  3.8 4.6 %margins.1 = (f32[8,48,128]{2,1,0:T(8,128)S(1)}, bf16[6144,512]{1,0:T(8,128)(2,1)S(1)}) custom-call(s32[48,128]{1,0:T(8,128)S(1)} %bitcast.4, s32[48,128]{1,0:T(8,128)S(1)} %bitcast.6, f32[64,128]{1,0:T(8,128)S(1)} %copy-done.1, bf16[512,128]{1,0:T(8,128)(2,1)S(1)} %copy-done, bf16[6144,512]{1,0:T(8,128)(2,1)} %q_hbm.1), custom_call_target="tpu_custom_call" | custom-call | flops 805306368 | bytes 6291456 | tf_op jit(solution)/shard_map/margins/pallas_call | solution.py:170
  8.4 17.8 %all_to_all.20.margins_ref = f32[8,48,128]{2,1,0:T(8,128)S(1)} all-to-all(f32[8,48,128]{2,1,0:T(8,128)S(1)} %get-tuple-element.12), channel_id=1, replica_groups=mesh['rows_0'=4,'rows_1'=4,'rows_2'=2,'feat'=8] {'feat'}, dimensions={0} | all-to-all | bytes 393216 | tf_op jit(solution)/shard_map/all_to_all | solution.py:23
  26.2 0.0 copy-done.4
  26.2 2.9 %grads.1 = (f32[32,9,2,128]{3,2,1,0:T(2,128)S(1)}, f32[48,128]{1,0:T(8,128)S(1)}) custom-call(f32[8,48,128]{2,1,0:T(8,128)S(1)} %all_to_all.20.margins_ref, s32[48,128]{1,0:T(8,128)S(1)} %bitcast.5, s32[48,128]{1,0:T(8,128)S(1)} %bitcast.7, s32[48,128]{1,0:T(8,128)S(1)} %bitcast.8, f32[64,128]{1,0:T(8,128)S(1)} %copy-done.1, bf16[512,128]{1,0:T(8,128)(2,1)S(1)} %copy-done, ...), custom_call_target="tpu_custom_call" | custom-call | flops 1610612736 | bytes 6291456 | tf_op jit(solution)/shard_map/grads/pallas_call | solution.py:170
  29.1 18.6 %all_to_all.21.parts_ref = f32[32,9,2,128]{3,2,1,0:T(2,128)S(1)} all-to-all(f32[32,9,2,128]{3,2,1,0:T(2,128)S(1)} %get-tuple-element.14), channel_id=1, replica_groups=mesh['rows_0'=4,'rows_1'=4,'rows_2'=2,'feat'=8] {'rows_0','rows_1','rows..., dimensions={0} | all-to-all | bytes 589824 | tf_op jit(solution)/shard_map/all_to_all | solution.py:23
  47.7 0.1 shares.1
  47.8 9.0 %all_to_all.22.parts_ref = f32[8,2,2,128]{3,2,1,0:T(2,128)S(1)} all-to-all(f32[8,2,2,128]{3,2,1,0:T(2,128)S(1)} %get-tuple-element.15), channel_id=1, replica_groups=mesh['rows_0'=4,'rows_1'=4,'rows_2'=2,'feat'=8] {'feat'}, dimensions={0} | all-to-all | bytes 32768 | tf_op jit(solution)/shard_map/all_to_all | solution.py:23
  56.8 0.1 pack.1
  56.9 14.2 %all_to_all.23.parts_ref = f32[32,10,2,128]{3,2,1,0:T(2,128)S(1)} all-to-all(f32[32,10,2,128]{3,2,1,0:T(2,128)S(1)} %pack.1), channel_id=1, replica_groups=mesh['rows_0'=4,'rows_1'=4,'rows_2'=2,'feat'=8] {'rows_0','rows_1','rows..., dimensions={0} | all-to-all | bytes 655360 | tf_op jit(solution)/shard_map/all_to_all | solution.py:23
  71.1 0.9 %final.1 = (f32[512,128]{1,0:T(8,128)}, f32[64,128]{1,0:T(8,128)}, f32[1,1]{1,0:T(1,128)}) custom-call(f32[32,10,2,128]{3,2,1,0:T(2,128)S(1)} %all_to_all.23.parts_ref), custom_call_target="tpu_custom_call" | custom-call | flops 10000 | bytes 600000 | tf_op jit(solution)/shard_map/final/pallas_call | solution.py:170
Async XLA Ops:
  0.6 0.9 %copy-start = (bf16[512,128]{1,0:T(8,128)(2,1)S(1)}, bf16[512,128]{1,0:T(8,128)(2,1)}, u32[]{:S(2)}) copy-start(bf16[512,128]{1,0:T(8,128)(2,1)} %proj_ref.3) | copy-start | bytes 393220
  1.5 0.8 %copy-start.1 = (f32[64,128]{1,0:T(8,128)S(1)}, f32[64,128]{1,0:T(8,128)}, u32[]{:S(2)}) copy-start(f32[64,128]{1,0:T(8,128)} %models_ref.3) | copy-start | bytes 98308
  2.3 0.7 %copy-start.2 = (s32[6144]{0:T(1024)S(1)}, s32[6144]{0:T(1024)}, u32[]{:S(2)}) copy-start(s32[6144]{0:T(1024)} %param.9) | copy-start | bytes 73732
  3.0 0.7 %copy-start.3 = (s32[6144]{0:T(1024)S(1)}, s32[6144]{0:T(1024)}, u32[]{:S(2)}) copy-start(s32[6144]{0:T(1024)} %param.10) | copy-start | bytes 73732
  3.8 22.4 %copy-start.4 = (s32[6144]{0:T(1024)S(1)}, s32[6144]{0:T(1024)}, u32[]{:S(2)}) copy-start(s32[6144]{0:T(1024)} %param.11) | copy-start | bytes 73732

commit v2 on v1

--- a/solution.py
+++ b/solution.py
@@ -16,7 +16,9 @@
 F32 = jnp.float32
 BF16 = jnp.bfloat16
 MIB = 1 << 20
-CHUNK = 1024
+BLOCK = 1024
+AHEAD = 4
+CHUNK = 2048
 
 
 def exchange(x, axis):
@@ -51,32 +53,39 @@
     return jnp.concatenate(tiles, axis=1)
 
 
-def gaps(table, pick):
-    pick = pick.astype(BF16)
-    return contract(table, jnp.concatenate([pick, pick, pick], axis=0), 1, 0)
-
-
-def margin_kernel(first_ref, second_ref, models_ref, proj_ref, q_hbm, out_ref, q_ref, sems):
-    tokens = q_hbm.shape[0]
-    copies = []
-    for i in range(tokens // CHUNK):
-        rows = pl.ds(i * CHUNK, CHUNK)
-        copies.append(pltpu.make_async_copy(q_hbm.at[rows, :], q_ref.at[rows, :], sems.at[i]))
-        copies[-1].start()
+def margin_kernel(first_hbm, second_hbm, models_hbm, proj_hbm, q_hbm, out_ref, q_ref, gap_ref, pick_ref, proj_ref, first_ref, second_ref, models_ref, q_sems, sems):
+    tokens = q_ref.shape[0]
+    small = [(models_hbm, models_ref), (first_hbm, first_ref), (second_hbm, second_ref), (proj_hbm, proj_ref)]
+    small = [pltpu.make_async_copy(a, b, sems.at[i]) for i, (a, b) in enumerate(small)]
+    for copy in small:
+        copy.start()
+    blocks = [pl.ds(i * BLOCK, BLOCK) for i in range(tokens // BLOCK)]
+    copies = [pltpu.make_async_copy(q_hbm.at[rows, :], q_ref.at[rows, :], q_sems.at[i]) for i, rows in enumerate(blocks)]
+    for copy in copies[:AHEAD]:
+        copy.start()
+    for copy in small[:3]:
+        copy.wait()
     table = model_table(models_ref[...])
+    for start in range(0, tokens, CHUNK):
+        pick = picks(first_ref, second_ref, start, CHUNK).astype(BF16)
+        pick_ref[:, start : start + CHUNK] = pick
+        gap_ref[:, start : start + CHUNK] = contract(table, jnp.concatenate([pick, pick, pick], axis=0), 1, 0)
+    small[3].wait()
     proj = proj_ref[...].astype(F32).T.astype(BF16)
-    for i in range(tokens // CHUNK):
-        gap = gaps(table, picks(first_ref, second_ref, i * CHUNK, CHUNK))
-        copies[i].wait()
-        routed = contract(proj, q_ref[pl.ds(i * CHUNK, CHUNK), :], 1, 1)
-        margin = jnp.sum(routed * gap, axis=0, keepdims=True)
+    for start in range(0, tokens, CHUNK):
+        for i in range(start // BLOCK, (start + CHUNK) // BLOCK):
+            copies[i].wait()
+            if i + AHEAD < len(copies):
+                copies[i + AHEAD].start()
+        routed = contract(proj, q_ref[start : start + CHUNK, :], 1, 1)
+        margin = jnp.sum(routed * gap_ref[:, start : start + CHUNK], axis=0, keepdims=True)
         for j in range(CHUNK // LANES):
             row = margin[:, j * LANES : (j + 1) * LANES]
             for k in range(out_ref.shape[0]):
-                out_ref[k, pl.ds(i * (CHUNK // LANES) + j, 1), :] = row
-
-
-def grad_kernel(total, share, margins_ref, first_ref, second_ref, wins_ref, models_ref, proj_ref, q_ref, out_ref, loss_ref, coef_ref, acc_ref):
+                out_ref[k, start // LANES + j : start // LANES + j + 1, :] = row
+
+
+def grad_kernel(total, share, margins_ref, wins_ref, gap_ref, pick_ref, proj_ref, q_ref, out_ref, loss_ref, coef_ref, acc_ref):
     tokens = q_ref.shape[0]
     margin = margins_ref[0]
     for k in range(1, margins_ref.shape[0]):
@@ -85,15 +94,14 @@
     wrong = -sign * margin
     loss_ref[...] = jax.nn.softplus(wrong) / total
     coef_ref[...] = -sign * jax.nn.sigmoid(wrong) / total
-    table = model_table(models_ref[...])
-    for i in range(tokens // CHUNK):
-        pick = picks(first_ref, second_ref, i * CHUNK, CHUNK)
-        gap = gaps(table, pick)
-        first_row = i * CHUNK // LANES
-        coef = jnp.concatenate([coef_ref[first_row + j : first_row + j + 1, :] for j in range(CHUNK // LANES)], axis=1)
-        left = jnp.concatenate([(coef * gap).astype(BF16), *pieces(coef * pick, 2)], axis=0)
-        part = contract(left, q_ref[pl.ds(i * CHUNK, CHUNK), :], 1, 0)
-        if i == 0:
+    for start in range(0, tokens, BLOCK):
+        cut = slice(start, start + BLOCK)
+        row = start // LANES
+        coef = jnp.concatenate([coef_ref[row + j : row + j + 1, :] for j in range(BLOCK // LANES)], axis=1)
+        back = (coef * gap_ref[:, cut]).astype(BF16)
+        left = jnp.concatenate([back, *pieces(coef * pick_ref[:, cut].astype(F32), 2)], axis=0)
+        part = contract(left, q_ref[cut, :], 1, 0)
+        if start == 0:
             acc_ref[...] = part
         else:
             acc_ref[...] += part
@@ -189,21 +197,34 @@
     share = width // rows
     kinds = NM // rows // 2
     first, second, wins = (x.reshape(tokens // LANES, LANES) for x in (first, second, wins))
-    margins, held = kernel_call(
+    sources = (first, second, models, projection, queries)
+    margins, held, gap, pick, proj = kernel_call(
         margin_kernel,
-        (shape(feats, tokens // LANES, LANES), pltpu.VMEM((tokens, width), BF16)),
-        (first, second, models, projection, pltpu.with_memory_space_constraint(queries, pltpu.HBM)),
+        (
+            shape(feats, tokens // LANES, LANES),
+            pltpu.VMEM((tokens, width), BF16),
+            pltpu.VMEM((R, tokens), F32),
+            pltpu.VMEM((NM, tokens), BF16),
+            pltpu.VMEM(projection.shape, BF16),
+        ),
+        [pltpu.with_memory_space_constraint(x, pltpu.HBM) for x in sources],
         "margins",
         24,
         (2 * tokens * width * R, tokens * width * 2),
-        in_specs=[VMEM] * 4 + [HBM],
-        scratch=[pltpu.SemaphoreType.DMA((tokens // CHUNK,))],
+        in_specs=[HBM] * len(sources),
+        scratch=[
+            pltpu.VMEM(first.shape, jnp.int32),
+            pltpu.VMEM(first.shape, jnp.int32),
+            pltpu.VMEM(models.shape, F32),
+            pltpu.SemaphoreType.DMA((tokens // BLOCK,)),
+            pltpu.SemaphoreType.DMA((4,)),
+        ],
     )
     margins = exchange(margins, "feat")
     parts, loss = kernel_call(
         functools.partial(grad_kernel, float(tokens * rows), share),
         (shape(rows, share // 2 + kinds, 2, LANES), shape(tokens // LANES, LANES)),
-        (margins, first, second, wins, models, projection, held),
+        (margins, wins, gap, pick, proj, held),
         "grads",
         24,
         (4 * tokens * width * R, tokens * width * 2),

time: 72.5 us -> 68.3 us (0.942)
  local copies, waits for them, and re-layouts: 3.13 us -> 0.01 us
  Pallas kernels: 8.64 us -> 7.82 us
    unnamed x10 -> x2, local copies, waits for them, and re-layouts: 3.13 us -> 0.01 us
    pallas_call x5, Pallas kernels: 8.64 us -> 7.82 us  [kernel_call(): pl.pallas_call(body, out_shape=outs, in_specs=in_specs or [VMEM] * len(in...]
where the time goes in v2:
time: 68.3 us; the launch traced here: 68.1 us
  blocking collectives  59.6 us (87%)
  Pallas kernels  7.82 us (11%)
    all_to_all x4, blocking collectives, exchange(): return lax.all_to_all(x, axis, split_axis=0, concat_axis=0, tiled=True)  59.6 us
    pallas_call x5, Pallas kernels, kernel_call(): pl.pallas_call(body, out_shape=outs, in_specs=in_specs or [VMEM] * len(in...  7.82 us

profile of v2, /device:TPU:1, one launch (start us, length us, event | category | flops | bytes accessed | tf_op | source)
XLA Modules:
  0.0 68.1 jit_solution(17886325716972809996)
XLA Ops:
  0.6 0.0 copy-start
  0.6 4.8 %margins.1 = (f32[8,48,128]{2,1,0:T(8,128)S(1)}, bf16[6144,512]{1,0:T(8,128)(2,1)S(1)}, f32[128,6144]{1,0:T(8,128)S(1)}, bf16[64,6144]{1,0:T(8,128)(2,1)S(1)}, bf16[512,128]{1,0:T(8,128)(2,1)S(1)}) custom-call(s32[48,128]{1,0:T(8,128)} %bitcast.5, s32[48,128]{1,0:T(8,128)} %bitcast.6, f32[64,128]{1,0:T(8,128)} %models_hbm.1, bf16[512,128]{1,0:T(8,128)(2,1)} %proj_hbm.1, ...), custom_call_target="tpu_custom_call" | custom-call | flops 805306368 | bytes 6291456 | tf_op jit(solution)/shard_map/margins/pallas_call | solution.py:178
  5.4 17.8 %all_to_all.20.margins_ref = f32[8,48,128]{2,1,0:T(8,128)S(1)} all-to-all(f32[8,48,128]{2,1,0:T(8,128)S(1)} %get-tuple-element.15), channel_id=1, replica_groups=mesh['rows_0'=4,'rows_1'=4,'rows_2'=2,'feat'=8] {'feat'}, dimensions={0} | all-to-all | bytes 393216 | tf_op jit(solution)/shard_map/all_to_all | solution.py:25
  23.2 0.0 copy-done
  23.2 2.0 %grads.1 = (f32[32,9,2,128]{3,2,1,0:T(2,128)S(1)}, f32[48,128]{1,0:T(8,128)S(1)}) custom-call(f32[8,48,128]{2,1,0:T(8,128)S(1)} %all_to_all.20.margins_ref, s32[48,128]{1,0:T(8,128)S(1)} %bitcast.4, f32[128,6144]{1,0:T(8,128)S(1)} %get-tuple-element.16.gap_ref, bf16[64,6144]{1,0:T(8,128)(2,1)S(1)} %get-tuple-element.17.pick_ref, ...), custom_call_target="tpu_custom_call" | custom-call | flops 1610612736 | bytes 6291456 | tf_op jit(solution)/shard_map/grads/pallas_call | solution.py:178
  25.2 18.6 %all_to_all.21.parts_ref = f32[32,9,2,128]{3,2,1,0:T(2,128)S(1)} all-to-all(f32[32,9,2,128]{3,2,1,0:T(2,128)S(1)} %get-tuple-element.20), channel_id=1, replica_groups=mesh['rows_0'=4,'rows_1'=4,'rows_2'=2,'feat'=8] {'rows_0','rows_1','rows..., dimensions={0} | all-to-all | bytes 589824 | tf_op jit(solution)/shard_map/all_to_all | solution.py:25
  43.8 0.1 shares.1
  43.9 9.0 %all_to_all.22.parts_ref = f32[8,2,2,128]{3,2,1,0:T(2,128)S(1)} all-to-all(f32[8,2,2,128]{3,2,1,0:T(2,128)S(1)} %get-tuple-element.21), channel_id=1, replica_groups=mesh['rows_0'=4,'rows_1'=4,'rows_2'=2,'feat'=8] {'feat'}, dimensions={0} | all-to-all | bytes 32768 | tf_op jit(solution)/shard_map/all_to_all | solution.py:25
  52.9 0.1 pack.1
  52.9 14.2 %all_to_all.23.parts_ref = f32[32,10,2,128]{3,2,1,0:T(2,128)S(1)} all-to-all(f32[32,10,2,128]{3,2,1,0:T(2,128)S(1)} %pack.1), channel_id=1, replica_groups=mesh['rows_0'=4,'rows_1'=4,'rows_2'=2,'feat'=8] {'rows_0','rows_1','rows..., dimensions={0} | all-to-all | bytes 655360 | tf_op jit(solution)/shard_map/all_to_all | solution.py:25
  67.2 0.9 %final.1 = (f32[512,128]{1,0:T(8,128)}, f32[64,128]{1,0:T(8,128)}, f32[1,1]{1,0:T(1,128)}) custom-call(f32[32,10,2,128]{3,2,1,0:T(2,128)S(1)} %all_to_all.23.parts_ref), custom_call_target="tpu_custom_call" | custom-call | flops 10000 | bytes 600000 | tf_op jit(solution)/shard_map/final/pallas_call | solution.py:178
Async XLA Ops:
  0.6 22.6 %copy-start = (s32[6144]{0:T(1024)S(1)}, s32[6144]{0:T(1024)}, u32[]{:S(2)}) copy-start(s32[6144]{0:T(1024)} %param.11) | copy-start | bytes 73732

commit v3 on v2

--- a/solution.py
+++ b/solution.py
@@ -17,7 +17,7 @@
 BF16 = jnp.bfloat16
 MIB = 1 << 20
 BLOCK = 1024
-AHEAD = 4
+AHEAD = 2
 CHUNK = 2048
 
 
@@ -66,17 +66,20 @@
     for copy in small[:3]:
         copy.wait()
     table = model_table(models_ref[...])
-    for start in range(0, tokens, CHUNK):
-        pick = picks(first_ref, second_ref, start, CHUNK).astype(BF16)
-        pick_ref[:, start : start + CHUNK] = pick
-        gap_ref[:, start : start + CHUNK] = contract(table, jnp.concatenate([pick, pick, pick], axis=0), 1, 0)
+    started = AHEAD
+    for start in range(0, tokens, BLOCK):
+        cut = slice(start, start + BLOCK)
+        pick = picks(first_ref, second_ref, start, BLOCK).astype(BF16)
+        pick_ref[:, cut] = pick
+        gap_ref[:, cut] = contract(table, jnp.concatenate([pick, pick, pick], axis=0), 1, 0)
+        if start > 0 and started < len(copies):
+            copies[started].start()
+            started += 1
     small[3].wait()
     proj = proj_ref[...].astype(F32).T.astype(BF16)
     for start in range(0, tokens, CHUNK):
         for i in range(start // BLOCK, (start + CHUNK) // BLOCK):
             copies[i].wait()
-            if i + AHEAD < len(copies):
-                copies[i + AHEAD].start()
         routed = contract(proj, q_ref[start : start + CHUNK, :], 1, 1)
         margin = jnp.sum(routed * gap_ref[:, start : start + CHUNK], axis=0, keepdims=True)
         for j in range(CHUNK // LANES):

time: 68.3 us -> 68.2 us (level)
  no operation moved by 1% of the time
where the time goes in v3:
time: 68.2 us; the launch traced here: 67.9 us
  blocking collectives  59.6 us (87%)
  Pallas kernels  7.67 us (11%)
    all_to_all x4, blocking collectives, exchange(): return lax.all_to_all(x, axis, split_axis=0, concat_axis=0, tiled=True)  59.6 us
    pallas_call x5, Pallas kernels, kernel_call(): pl.pallas_call(body, out_shape=outs, in_specs=in_specs or [VMEM] * len(in...  7.67 us

profile of v3, /device:TPU:1, one launch (start us, length us, event | category | flops | bytes accessed | tf_op | source)
XLA Modules:
  0.0 67.9 jit_solution(13695080225197625132)
XLA Ops:
  0.6 0.0 copy-start
  0.6 4.6 %margins.1 = (f32[8,48,128]{2,1,0:T(8,128)S(1)}, bf16[6144,512]{1,0:T(8,128)(2,1)S(1)}, f32[128,6144]{1,0:T(8,128)S(1)}, bf16[64,6144]{1,0:T(8,128)(2,1)S(1)}, bf16[512,128]{1,0:T(8,128)(2,1)S(1)}) custom-call(s32[48,128]{1,0:T(8,128)} %bitcast.5, s32[48,128]{1,0:T(8,128)} %bitcast.6, f32[64,128]{1,0:T(8,128)} %models_hbm.1, bf16[512,128]{1,0:T(8,128)(2,1)} %proj_hbm.1, ...), custom_call_target="tpu_custom_call" | custom-call | flops 805306368 | bytes 6291456 | tf_op jit(solution)/shard_map/margins/pallas_call | solution.py:181
  5.3 17.8 %all_to_all.20.margins_ref = f32[8,48,128]{2,1,0:T(8,128)S(1)} all-to-all(f32[8,48,128]{2,1,0:T(8,128)S(1)} %get-tuple-element.15), channel_id=1, replica_groups=mesh['rows_0'=4,'rows_1'=4,'rows_2'=2,'feat'=8] {'feat'}, dimensions={0} | all-to-all | bytes 393216 | tf_op jit(solution)/shard_map/all_to_all | solution.py:25
  23.1 0.0 copy-done
  23.1 2.0 %grads.1 = (f32[32,9,2,128]{3,2,1,0:T(2,128)S(1)}, f32[48,128]{1,0:T(8,128)S(1)}) custom-call(f32[8,48,128]{2,1,0:T(8,128)S(1)} %all_to_all.20.margins_ref, s32[48,128]{1,0:T(8,128)S(1)} %bitcast.4, f32[128,6144]{1,0:T(8,128)S(1)} %get-tuple-element.16.gap_ref, bf16[64,6144]{1,0:T(8,128)(2,1)S(1)} %get-tuple-element.17.pick_ref, ...), custom_call_target="tpu_custom_call" | custom-call | flops 1610612736 | bytes 6291456 | tf_op jit(solution)/shard_map/grads/pallas_call | solution.py:181
  25.0 18.6 %all_to_all.21.parts_ref = f32[32,9,2,128]{3,2,1,0:T(2,128)S(1)} all-to-all(f32[32,9,2,128]{3,2,1,0:T(2,128)S(1)} %get-tuple-element.20), channel_id=1, replica_groups=mesh['rows_0'=4,'rows_1'=4,'rows_2'=2,'feat'=8] {'rows_0','rows_1','rows..., dimensions={0} | all-to-all | bytes 589824 | tf_op jit(solution)/shard_map/all_to_all | solution.py:25
  43.6 0.1 shares.1
  43.7 9.0 %all_to_all.22.parts_ref = f32[8,2,2,128]{3,2,1,0:T(2,128)S(1)} all-to-all(f32[8,2,2,128]{3,2,1,0:T(2,128)S(1)} %get-tuple-element.21), channel_id=1, replica_groups=mesh['rows_0'=4,'rows_1'=4,'rows_2'=2,'feat'=8] {'feat'}, dimensions={0} | all-to-all | bytes 32768 | tf_op jit(solution)/shard_map/all_to_all | solution.py:25
  52.7 0.1 pack.1
  52.8 14.2 %all_to_all.23.parts_ref = f32[32,10,2,128]{3,2,1,0:T(2,128)S(1)} all-to-all(f32[32,10,2,128]{3,2,1,0:T(2,128)S(1)} %pack.1), channel_id=1, replica_groups=mesh['rows_0'=4,'rows_1'=4,'rows_2'=2,'feat'=8] {'rows_0','rows_1','rows..., dimensions={0} | all-to-all | bytes 655360 | tf_op jit(solution)/shard_map/all_to_all | solution.py:25
  67.0 0.9 %final.1 = (f32[512,128]{1,0:T(8,128)}, f32[64,128]{1,0:T(8,128)}, f32[1,1]{1,0:T(1,128)}) custom-call(f32[32,10,2,128]{3,2,1,0:T(2,128)S(1)} %all_to_all.23.parts_ref), custom_call_target="tpu_custom_call" | custom-call | flops 10000 | bytes 600000 | tf_op jit(solution)/shard_map/final/pallas_call | solution.py:181
Async XLA Ops:
  0.6 22.4 %copy-start = (s32[6144]{0:T(1024)S(1)}, s32[6144]{0:T(1024)}, u32[]{:S(2)}) copy-start(s32[6144]{0:T(1024)} %param.11) | copy-start | bytes 73732

commit v4 on v3

--- a/solution.py
+++ b/solution.py
@@ -12,7 +12,9 @@
 R = 128
 NM = 64
 LANES = 128
-ROWS = ("rows_0", "rows_1", "rows_2")
+CORE = "rows_2"
+CHIPS = ("rows_0", "rows_1")
+ROWS = (*CHIPS, CORE)
 F32 = jnp.float32
 BF16 = jnp.bfloat16
 MIB = 1 << 20
@@ -23,6 +25,10 @@
 
 def exchange(x, axis):
     return lax.all_to_all(x, axis, split_axis=0, concat_axis=0, tiled=True)
+
+
+def swap(x):
+    return lax.ppermute(x, CORE, [(0, 1), (1, 0)])
 
 
 def pieces(x, count):
@@ -51,6 +57,11 @@
         two = jnp.where(labels == second_ref[i : i + 1, :], 1.0, 0.0)
         tiles.append(one - two)
     return jnp.concatenate(tiles, axis=1)
+
+
+def halve(x, flip):
+    half = x.shape[0] // 2
+    return jnp.where(flip, x[half:], x[:half]), jnp.where(flip, x[:half], x[half:])
 
 
 def margin_kernel(first_hbm, second_hbm, models_hbm, proj_hbm, q_hbm, out_ref, q_ref, gap_ref, pick_ref, proj_ref, first_ref, second_ref, models_ref, q_sems, sems):
@@ -88,7 +99,7 @@
                 out_ref[k, start // LANES + j : start // LANES + j + 1, :] = row
 
 
-def grad_kernel(total, share, margins_ref, wins_ref, gap_ref, pick_ref, proj_ref, q_ref, out_ref, loss_ref, coef_ref, acc_ref):
+def grad_kernel(total, share, margins_ref, wins_ref, gap_ref, pick_ref, proj_ref, q_ref, own_ref, other_ref, loss_ref, coef_ref, acc_ref):
     tokens = q_ref.shape[0]
     margin = margins_ref[0]
     for k in range(1, margins_ref.shape[0]):
@@ -112,14 +123,17 @@
     weighted = acc_ref[R : R + NM, :] + acc_ref[R + NM :, :]
     model_terms = contract(jnp.concatenate(pieces(weighted, 3), axis=0), proj_ref[...], 1, 0)
     model_grad = model_terms[:NM] + model_terms[NM : 2 * NM] + model_terms[2 * NM :]
-    count = out_ref.shape[0]
-    for j in range(count):
-        for i in range(share // 2):
-            at = j * share + 2 * i
-            out_ref[j, i] = grad[at : at + 2]
-        for i in range(NM // count // 2):
-            at = j * (NM // count) + 2 * i
-            out_ref[j, share // 2 + i] = model_grad[at : at + 2]
+    flip = lax.axis_index(CORE) == 1
+    halves = [halve(x, flip) for x in (grad, model_grad)]
+    count = own_ref.shape[0]
+    for ref, grad, model_grad in zip((own_ref, other_ref), *halves):
+        for j in range(count):
+            for i in range(share // 2):
+                at = j * share + 2 * i
+                ref[j, i] = grad[at : at + 2]
+            for i in range(NM // 2 // count // 2):
+                at = j * (NM // 2 // count) + 2 * i
+                ref[j, share // 2 + i] = model_grad[at : at + 2]
 
 
 def share_kernel(parts_ref, share_ref, out_ref):
@@ -153,23 +167,28 @@
         out_ref[k, pairs + kinds, 1:2] = loss
 
 
-def final_kernel(share, parts_ref, proj_ref, models_ref, loss_ref):
-    count, entries = parts_ref.shape[0], parts_ref.shape[1]
+def final_kernel(share, own_ref, other_ref, proj_ref, models_ref, loss_ref):
+    count, entries = own_ref.shape[0], own_ref.shape[1]
     pairs = share // 2
     kinds = entries - pairs - 1
-    sums = parts_ref[0, entries - 1]
+    sums = own_ref[0, entries - 1] + other_ref[0, entries - 1]
     for k in range(1, count):
-        sums = sums + parts_ref[k, entries - 1]
+        sums = sums + (own_ref[k, entries - 1] + other_ref[k, entries - 1])
     sums = jnp.sum(sums, axis=1, keepdims=True)
     loss_ref[...] = sums[1:2]
     scale = jnp.sqrt(F32(D * R + NM * R)) / (jnp.sqrt(sums[0:1]) + 1e-06)
     scale = jnp.broadcast_to(scale, (2, LANES))
+    flip = lax.axis_index(CORE) == 1
     for k in range(count):
-        for i in range(pairs):
-            proj_ref[k * share + 2 * i : k * share + 2 * i + 2, :] = scale * parts_ref[k, i]
-        for i in range(kinds):
-            at = 2 * (k * kinds + i)
-            models_ref[at : at + 2, :] = scale * parts_ref[k, pairs + i]
+        for i in range(pairs + kinds):
+            own, other = scale * own_ref[k, i], scale * other_ref[k, i]
+            for c, rows in enumerate((jnp.where(flip, other, own), jnp.where(flip, own, other))):
+                if i < pairs:
+                    at = (c * count + k) * share + 2 * i
+                    proj_ref[at : at + 2, :] = rows
+                else:
+                    at = 2 * ((c * count + k) * kinds + i - pairs)
+                    models_ref[at : at + 2, :] = rows
 
 
 VMEM = pl.BlockSpec(memory_space=pltpu.VMEM)
@@ -196,7 +215,7 @@
 
 def body(queries, projection, models, first, second, wins):
     tokens, width = queries.shape
-    rows, feats = lax.axis_size(ROWS), lax.axis_size("feat")
+    rows, chips, feats = lax.axis_size(ROWS), lax.axis_size(CHIPS), lax.axis_size("feat")
     share = width // rows
     kinds = NM // rows // 2
     first, second, wins = (x.reshape(tokens // LANES, LANES) for x in (first, second, wins))
@@ -224,16 +243,17 @@
         ],
     )
     margins = exchange(margins, "feat")
-    parts, loss = kernel_call(
+    packed = shape(chips, share // 2 + kinds, 2, LANES)
+    own, other, loss = kernel_call(
         functools.partial(grad_kernel, float(tokens * rows), share),
-        (shape(rows, share // 2 + kinds, 2, LANES), shape(tokens // LANES, LANES)),
+        (packed, packed, shape(tokens // LANES, LANES)),
         (margins, wins, gap, pick, proj, held),
         "grads",
         24,
         (4 * tokens * width * R, tokens * width * 2),
         scratch=[pltpu.VMEM((tokens // LANES, LANES), F32), pltpu.VMEM((R + 2 * NM, width), F32)],
     )
-    parts = exchange(parts, ROWS)
+    parts = exchange(own + swap(other), CHIPS)
     grad_share, parts = kernel_call(
         share_kernel,
         (shape(share // 2, 2, LANES), shape(feats, kinds + 1, 2, LANES)),
@@ -245,17 +265,17 @@
     parts = exchange(parts, "feat")
     parts = kernel_call(
         pack_kernel,
-        shape(rows, share // 2 + kinds + 1, 2, LANES),
+        shape(chips, share // 2 + kinds + 1, 2, LANES),
         (parts, grad_share, loss),
         "pack",
         4,
         (10000, 400000),
     )
-    parts = exchange(parts, ROWS)
+    parts = exchange(parts, CHIPS)
     update_proj, update_models, loss = kernel_call(
         functools.partial(final_kernel, share),
         (shape(width, R), shape(NM, R), shape(1, 1)),
-        (parts,),
+        (parts, swap(parts)),
         "final",
         4,
         (10000, 600000),

time: 68.2 us -> 67.5 us (0.990)
  blocking collectives: 59.6 us -> 50.3 us
  starting transfers between devices: 0 us -> 6.6 us
  waiting for transfers between devices: 0 us -> 2.04 us
    all_to_all x4, blocking collectives: 59.6 us -> 50.3 us  [exchange(): return lax.all_to_all(x, axis, split_axis=0, concat_axis=0, tiled=True)]
    ppermute x0 -> x2, starting transfers between devices: none -> 6.6 us  [swap(): return lax.ppermute(x, CORE, [(0, 1), (1, 0)])]
    ppermute x0 -> x2, waiting for transfers between devices: none -> 2.04 us  [swap(): return lax.ppermute(x, CORE, [(0, 1), (1, 0)])]
  transfers between devices with their start and end apart: 0 -> 2, of which waited for: 0 -> 2; matrix products, arithmetic and copies ran while one was open for 0% -> 0% of each run, Pallas kernels for 0% -> 0%
where the time goes in v4:
time: 67.5 us; the launch traced here: 67.3 us
  blocking collectives  50.3 us (75%)
  Pallas kernels  7.58 us (11%)
  starting transfers between devices  6.6 us (10%)
  waiting for transfers between devices  2.04 us (3%)
    all_to_all x4, blocking collectives, exchange(): return lax.all_to_all(x, axis, split_axis=0, concat_axis=0, tiled=True)  50.3 us
    pallas_call x5, Pallas kernels, kernel_call(): pl.pallas_call(body, out_shape=outs, in_specs=in_specs or [VMEM] * len(in...  7.58 us
    ppermute x2, starting transfers between devices, swap(): return lax.ppermute(x, CORE, [(0, 1), (1, 0)])  6.6 us
    ppermute x2, waiting for transfers between devices, swap(): return lax.ppermute(x, CORE, [(0, 1), (1, 0)])  2.04 us
  transfers between devices with their start and end apart: 2, of which 2 were waited for; matrix products, arithmetic and copies ran while one was open for 0% of the time, Pallas kernels for 0%

profile of v4, /device:TPU:1, one launch (start us, length us, event | category | flops | bytes accessed | tf_op | source)
XLA Modules:
  0.0 67.3 jit_solution(880456656527288741)
XLA Ops:
  0.6 0.0 copy-start
  0.6 4.6 %margins.1 = (f32[8,48,128]{2,1,0:T(8,128)S(1)}, bf16[6144,512]{1,0:T(8,128)(2,1)S(1)}, f32[128,6144]{1,0:T(8,128)S(1)}, bf16[64,6144]{1,0:T(8,128)(2,1)S(1)}, bf16[512,128]{1,0:T(8,128)(2,1)S(1)}) custom-call(s32[48,128]{1,0:T(8,128)} %bitcast.5, s32[48,128]{1,0:T(8,128)} %bitcast.6, f32[64,128]{1,0:T(8,128)} %models_hbm.1, bf16[512,128]{1,0:T(8,128)(2,1)} %proj_hbm.1, ...), custom_call_target="tpu_custom_call" | custom-call | flops 805306368 | bytes 6291456 | tf_op jit(solution)/shard_map/margins/pallas_call | solution.py:200
  5.3 17.8 %all_to_all.20.margins_ref = f32[8,48,128]{2,1,0:T(8,128)S(1)} all-to-all(f32[8,48,128]{2,1,0:T(8,128)S(1)} %get-tuple-element.16), channel_id=1, replica_groups=mesh['rows_0'=4,'rows_1'=4,'rows_2'=2,'feat'=8] {'feat'}, dimensions={0} | all-to-all | bytes 393216 | tf_op jit(solution)/shard_map/all_to_all | solution.py:27
  23.1 0.0 copy-done
  23.1 2.0 %grads.1 = (f32[16,9,2,128]{3,2,1,0:T(2,128)S(1)}, f32[16,9,2,128]{3,2,1,0:T(2,128)S(1)}, f32[48,128]{1,0:T(8,128)S(1)}) custom-call(f32[8,48,128]{2,1,0:T(8,128)S(1)} %all_to_all.20.margins_ref, s32[48,128]{1,0:T(8,128)S(1)} %bitcast.4, f32[128,6144]{1,0:T(8,128)S(1)} %get-tuple-element.17.gap_ref, bf16[64,6144]{1,0:T(8,128)(2,1)S(1)} %get-tuple-element.18.pick_ref, ...), custom_call_target="tpu_custom_call" | custom-call | flops 1610612736 | bytes 6291456 | tf_op jit(solution)/shard_map/grads/pallas_call | solution.py:200
  25.0 2.5 %collective-permute-start = (f32[16,9,2,128]{3,2,1,0:T(2,128)S(1)}, f32[16,9,2,128]{3,2,1,0:T(2,128)S(1)}, u32[]{:S(2)}, u32[]{:S(2)}) collective-permute-start(f32[16,9,2,128]{3,2,1,0:T(2,128)S(1)} %get-tuple-element.22), channel_id=1, source_target_pairs={{0,8},{8,0},{1,9},{9,1},{2,10},{10,2},{3,11},{11,3},{4,12},{12,4},... | collective-permute-start | bytes 442376 | tf_op jit(solution)/shard_map/ppermute | solution.py:31
  27.5 1.0 %collective-permute-done = f32[16,9,2,128]{3,2,1,0:T(2,128)S(1)} collective-permute-done((f32[16,9,2,128]{3,2,1,0:T(2,128)S(1)}, f32[16,9,2,128]{3,2,1,0:T(2,128)S(1)}, u32[]{:S(2)}, u32[]{:S(2)}) %collective-permute-start) | collective-permute-done | bytes 147488 | tf_op jit(solution)/shard_map/ppermute | solution.py:31
  28.6 0.1 add.3
  28.6 13.3 %all_to_all.21.parts_ref = f32[16,9,2,128]{3,2,1,0:T(2,128)S(1)} all-to-all(f32[16,9,2,128]{3,2,1,0:T(2,128)S(1)} %add.3), channel_id=1, replica_groups=mesh['rows_0'=4,'rows_1'=4,'rows_2'=2,'feat'=8] {'rows_0','rows_1'}, dimensions={0} | all-to-all | bytes 294912 | tf_op jit(solution)/shard_map/all_to_all | solution.py:27
  42.0 9.0 %all_to_all.22.parts_ref = f32[8,2,2,128]{3,2,1,0:T(2,128)S(1)} all-to-all(f32[8,2,2,128]{3,2,1,0:T(2,128)S(1)} %get-tuple-element.23), channel_id=1, replica_groups=mesh['rows_0'=4,'rows_1'=4,'rows_2'=2,'feat'=8] {'feat'}, dimensions={0} | all-to-all | bytes 32768 | tf_op jit(solution)/shard_map/all_to_all | solution.py:27
  51.0 10.3 %all_to_all.23.own_ref = f32[16,10,2,128]{3,2,1,0:T(2,128)S(1)} all-to-all(f32[16,10,2,128]{3,2,1,0:T(2,128)S(1)} %pack.1), channel_id=1, replica_groups=mesh['rows_0'=4,'rows_1'=4,'rows_2'=2,'feat'=8] {'rows_0','rows_1'}, dimensions={0} | all-to-all | bytes 327680 | tf_op jit(solution)/shard_map/all_to_all | solution.py:27
  61.3 4.1 %collective-permute-start.1 = (f32[16,10,2,128]{3,2,1,0:T(2,128)S(1)}, f32[16,10,2,128]{3,2,1,0:T(2,128)S(1)}, u32[]{:S(2)}, u32[]{:S(2)}) collective-permute-start(f32[16,10,2,128]{3,2,1,0:T(2,128)S(1)} %all_to_all.23.own_ref), channel_id=1, source_target_pairs={{0,8},{8,0},{1,9},{9,1},{2,10},{10,2},{3,11},{11,3},{4,12},{12,4},... | collective-permute-start | bytes 491528 | tf_op jit(solution)/shard_map/ppermute | solution.py:31
  65.3 1.0 %collective-permute-done.1.other_ref = f32[16,10,2,128]{3,2,1,0:T(2,128)S(1)} collective-permute-done((f32[16,10,2,128]{3,2,1,0:T(2,128)S(1)}, f32[16,10,2,128]{3,2,1,0:T(2,128)S(1)}, u32[]{:S(2)}, u32[]{:S(2)}) %collective-permute-start.1) | collective-permute-done | bytes 163872 | tf_op jit(solution)/shard_map/ppermute | solution.py:31
  66.4 0.9 %final.1 = (f32[512,128]{1,0:T(8,128)}, f32[64,128]{1,0:T(8,128)}, f32[1,1]{1,0:T(1,128)}) custom-call(f32[16,10,2,128]{3,2,1,0:T(2,128)S(1)} %all_to_all.23.own_ref, f32[16,10,2,128]{3,2,1,0:T(2,128)S(1)} %collective-permute-done.1.other_ref), custom_call_target="tpu_custom_call" | custom-call | flops 10000 | bytes 600000 | tf_op jit(solution)/shard_map/final/pallas_call | solution.py:200
  (2 shorter events, 0.1 us)
Async XLA Ops:
  0.6 22.4 %copy-start = (s32[6144]{0:T(1024)S(1)}, s32[6144]{0:T(1024)}, u32[]{:S(2)}) copy-start(s32[6144]{0:T(1024)} %param.11) | copy-start | bytes 73732
  25.0 3.5 %collective-permute-start = (f32[16,9,2,128]{3,2,1,0:T(2,128)S(1)}, f32[16,9,2,128]{3,2,1,0:T(2,128)S(1)}, u32[]{:S(2)}, u32[]{:S(2)}) collective-permute-start(f32[16,9,2,128]{3,2,1,0:T(2,128)S(1)} %get-tuple-element.22), channel_id=1, source_target_pairs={{0,8},{8,0},{1,9},{9,1},{2,10},{10,2},{3,11},{11,3},{4,12},{12,4},... | collective-permute-start | bytes 442376 | tf_op jit(solution)/shard_map/ppermute | solution.py:31
  61.3 5.1 %collective-permute-start.1 = (f32[16,10,2,128]{3,2,1,0:T(2,128)S(1)}, f32[16,10,2,128]{3,2,1,0:T(2,128)S(1)}, u32[]{:S(2)}, u32[]{:S(2)}) collective-permute-start(f32[16,10,2,128]{3,2,1,0:T(2,128)S(1)} %all_to_all.23.own_ref), channel_id=1, source_target_pairs={{0,8},{8,0},{1,9},{9,1},{2,10},{10,2},{3,11},{11,3},{4,12},{12,4},... | collective-permute-start | bytes 491528 | tf_op jit(solution)/shard_map/ppermute | solution.py:31

commit v5 on v3

--- a/solution.py
+++ b/solution.py
@@ -8,11 +8,14 @@
 from jax.sharding import Mesh
 from jax.sharding import PartitionSpec as P
 
+
 D = 4096
 R = 128
 NM = 64
 LANES = 128
-ROWS = ("rows_0", "rows_1", "rows_2")
+CORE = "rows_2"
+CHIPS = ("rows_0", "rows_1")
+ROWS = (*CHIPS, CORE)
 F32 = jnp.float32
 BF16 = jnp.bfloat16
 MIB = 1 << 20
@@ -23,6 +26,10 @@
 
 def exchange(x, axis):
     return lax.all_to_all(x, axis, split_axis=0, concat_axis=0, tiled=True)
+
+
+def swap(x):
+    return lax.ppermute(x, CORE, [(0, 1), (1, 0)])
 
 
 def pieces(x, count):
@@ -88,8 +95,22 @@
                 out_ref[k, start // LANES + j : start // LANES + j + 1, :] = row
 
 
-def grad_kernel(total, share, margins_ref, wins_ref, gap_ref, pick_ref, proj_ref, q_ref, out_ref, loss_ref, coef_ref, acc_ref):
+def put_pairs(ref, at, rows):
+    count = ref.shape[0]
+    pairs = rows.shape[0] // count // 2
+    for j in range(count):
+        for i in range(pairs):
+            row = 2 * (j * pairs + i)
+            ref[j, at + i] = rows[row : row + 2]
+
+
+def columns(half, width):
+    return pl.ds(pl.multiple_of(half * width, width), width)
+
+
+def other_kernel(total, margins_ref, wins_ref, gap_ref, pick_ref, q_ref, out_ref, loss_ref, left_ref, weighted_ref, coef_ref, acc_ref):
     tokens = q_ref.shape[0]
+    width = acc_ref.shape[1]
     margin = margins_ref[0]
     for k in range(1, margins_ref.shape[0]):
         margin = margin + margins_ref[k]
@@ -97,86 +118,109 @@
     wrong = -sign * margin
     loss_ref[...] = jax.nn.softplus(wrong) / total
     coef_ref[...] = -sign * jax.nn.sigmoid(wrong) / total
+    other = columns(1 - lax.axis_index(CORE), width)
     for start in range(0, tokens, BLOCK):
         cut = slice(start, start + BLOCK)
         row = start // LANES
         coef = jnp.concatenate([coef_ref[row + j : row + j + 1, :] for j in range(BLOCK // LANES)], axis=1)
         back = (coef * gap_ref[:, cut]).astype(BF16)
         left = jnp.concatenate([back, *pieces(coef * pick_ref[:, cut].astype(F32), 2)], axis=0)
-        part = contract(left, q_ref[cut, :], 1, 0)
+        left_ref[:, cut] = left
+        part = contract(left, q_ref[cut, other], 1, 0)
         if start == 0:
             acc_ref[...] = part
         else:
             acc_ref[...] += part
-    grad = acc_ref[:R, :].T
-    weighted = acc_ref[R : R + NM, :] + acc_ref[R + NM :, :]
-    model_terms = contract(jnp.concatenate(pieces(weighted, 3), axis=0), proj_ref[...], 1, 0)
-    model_grad = model_terms[:NM] + model_terms[NM : 2 * NM] + model_terms[2 * NM :]
-    count = out_ref.shape[0]
-    for j in range(count):
-        for i in range(share // 2):
-            at = j * share + 2 * i
-            out_ref[j, i] = grad[at : at + 2]
-        for i in range(NM // count // 2):
-            at = j * (NM // count) + 2 * i
-            out_ref[j, share // 2 + i] = model_grad[at : at + 2]
-
-
-def share_kernel(parts_ref, share_ref, out_ref):
+    put_pairs(out_ref, 0, acc_ref[:R, :].T)
+    weighted_ref[...] = acc_ref[R : R + NM, :] + acc_ref[R + NM :, :]
+
+
+def own_kernel(left_ref, weighted_ref, proj_ref, q_ref, out_ref, models_ref):
+    width = weighted_ref.shape[1]
+    core = lax.axis_index(CORE)
+    acc = contract(left_ref[...], q_ref[:, columns(core, width)], 1, 0)
+    put_pairs(out_ref, 0, acc[:R].T)
+    model_grad = jnp.zeros((NM, R), F32)
+    for half, weighted in ((core, acc[R : R + NM] + acc[R + NM :]), (1 - core, weighted_ref[...])):
+        terms = contract(jnp.concatenate(pieces(weighted, 3), axis=0), proj_ref[columns(half, width), :], 1, 0)
+        model_grad = model_grad + (terms[:NM] + terms[NM : 2 * NM] + terms[2 * NM :])
+    put_pairs(models_ref, 0, model_grad)
+
+
+def join_kernel(own_ref, other_ref, models_ref, out_ref):
+    pairs = own_ref.shape[1]
+    out_ref[:, :pairs] = own_ref[...] + other_ref[...]
+    out_ref[:, pairs:] = models_ref[...]
+
+
+def share_kernel(feats, parts_ref, loss_ref, share_ref, out_ref):
     summed = parts_ref[0]
     for k in range(1, parts_ref.shape[0]):
         summed = summed + parts_ref[k]
     pairs = share_ref.shape[0]
+    kinds = summed.shape[0] - pairs
     grad = summed[:pairs]
     share_ref[...] = grad
-    square = jnp.sum(grad * grad, axis=0)
+    square = jnp.sum(jnp.sum(grad * grad, axis=0), axis=0, keepdims=True)
+    loss = jnp.sum(loss_ref[...], axis=0, keepdims=True) / feats
     for k in range(out_ref.shape[0]):
-        out_ref[k, : summed.shape[0] - pairs] = summed[pairs:]
-        out_ref[k, summed.shape[0] - pairs] = square
-
-
-def pack_kernel(parts_ref, share_ref, loss_ref, out_ref):
+        out_ref[k, :kinds] = summed[pairs:]
+        out_ref[k, kinds, 0:1] = square
+        out_ref[k, kinds, 1:2] = loss
+
+
+def sum_kernel(parts_ref, out_ref):
     summed = parts_ref[0]
     for k in range(1, parts_ref.shape[0]):
         summed = summed + parts_ref[k]
-    pairs = share_ref.shape[0]
-    kinds = summed.shape[0] - 1
-    model_grad = summed[:kinds]
-    square = summed[kinds] + jnp.sum(model_grad * model_grad, axis=0)
-    square = jnp.sum(square, axis=0, keepdims=True)
-    loss = jnp.sum(loss_ref[...], axis=0, keepdims=True)
-    grad = share_ref[...]
-    for k in range(out_ref.shape[0]):
-        out_ref[k, :pairs] = grad
-        out_ref[k, pairs : pairs + kinds] = model_grad
-        out_ref[k, pairs + kinds, 0:1] = square
-        out_ref[k, pairs + kinds, 1:2] = loss
-
-
-def final_kernel(share, parts_ref, proj_ref, models_ref, loss_ref):
-    count, entries = parts_ref.shape[0], parts_ref.shape[1]
-    pairs = share // 2
-    kinds = entries - pairs - 1
-    sums = parts_ref[0, entries - 1]
+    out_ref[...] = summed
+
+
+def pack_kernel(summed_ref, own_ref, other_ref, out_ref):
+    kinds = summed_ref.shape[0] - 1
+    pairs = own_ref.shape[0]
+    model_grad, sums = summed_ref[:kinds], summed_ref[kinds]
+    flip = lax.axis_index(CORE) == 1
+    own, other = own_ref[...], other_ref[...]
+    at = 0
+    for share in (jnp.where(flip, other, own), jnp.where(flip, own, other)):
+        for i in range(pairs):
+            out_ref[0, at : at + 2, :] = share[i]
+            at += 2
+    for i in range(kinds):
+        out_ref[0, at : at + 2, :] = model_grad[i]
+        at += 2
+    square = jnp.sum(jnp.sum(model_grad * model_grad, axis=0), axis=0, keepdims=True)
+    out_ref[0, at : at + 1, :] = sums[0:1] + square
+    out_ref[0, at + 1 : at + 2, :] = sums[1:2]
+    if at + 2 < out_ref.shape[1]:
+        out_ref[0, at + 2 :, :] = jnp.zeros((out_ref.shape[1] - at - 2, LANES), F32)
+    packed = out_ref[0]
+    for k in range(1, out_ref.shape[0]):
+        out_ref[k] = packed
+
+
+def final_kernel(share, kinds, parts_ref, proj_ref, models_ref, loss_ref):
+    count = parts_ref.shape[0]
+    sums = parts_ref[0, 2 * share :, :]
     for k in range(1, count):
-        sums = sums + parts_ref[k, entries - 1]
+        sums = sums + parts_ref[k, 2 * share :, :]
     sums = jnp.sum(sums, axis=1, keepdims=True)
-    loss_ref[...] = sums[1:2]
-    scale = jnp.sqrt(F32(D * R + NM * R)) / (jnp.sqrt(sums[0:1]) + 1e-06)
-    scale = jnp.broadcast_to(scale, (2, LANES))
+    square, loss = (sums[kinds + i : kinds + i + 1] for i in range(2))
+    loss_ref[...] = loss
+    scale = jnp.sqrt(F32(D * R + NM * R)) / (jnp.sqrt(square) + 1e-06)
     for k in range(count):
-        for i in range(pairs):
-            proj_ref[k * share + 2 * i : k * share + 2 * i + 2, :] = scale * parts_ref[k, i]
-        for i in range(kinds):
-            at = 2 * (k * kinds + i)
-            models_ref[at : at + 2, :] = scale * parts_ref[k, pairs + i]
+        for c in range(2):
+            to = (c * count + k) * share
+            proj_ref[to : to + share, :] = scale * parts_ref[k, c * share : (c + 1) * share, :]
+        models_ref[k * kinds : (k + 1) * kinds, :] = scale * parts_ref[k, 2 * share : 2 * share + kinds, :]
 
 
 VMEM = pl.BlockSpec(memory_space=pltpu.VMEM)
 HBM = pl.BlockSpec(memory_space=pltpu.HBM)
 
 
-def kernel_call(body, outs, ins, name, limit, cost, in_specs=None, scratch=()):
+def kernel_call(body, outs, ins, limit, cost, in_specs=None, scratch=()):
     flops, moved = cost
     return pl.pallas_call(
         body,
@@ -186,7 +230,6 @@
         scratch_shapes=scratch,
         compiler_params=pltpu.CompilerParams(vmem_limit_bytes=limit * MIB),
         cost_estimate=pl.CostEstimate(flops=flops, bytes_accessed=moved, transcendentals=0),
-        name=name,
     )(*ins)
 
 
@@ -196,9 +239,9 @@
 
 def body(queries, projection, models, first, second, wins):
     tokens, width = queries.shape
-    rows, feats = lax.axis_size(ROWS), lax.axis_size("feat")
+    rows, chips, feats = lax.axis_size(ROWS), lax.axis_size(CHIPS), lax.axis_size("feat")
     share = width // rows
-    kinds = NM // rows // 2
+    kinds = NM // chips
     first, second, wins = (x.reshape(tokens // LANES, LANES) for x in (first, second, wins))
     sources = (first, second, models, projection, queries)
     margins, held, gap, pick, proj = kernel_call(
@@ -211,7 +254,6 @@
             pltpu.VMEM(projection.shape, BF16),
         ),
         [pltpu.with_memory_space_constraint(x, pltpu.HBM) for x in sources],
-        "margins",
         24,
         (2 * tokens * width * R, tokens * width * 2),
         in_specs=[HBM] * len(sources),
@@ -224,39 +266,51 @@
         ],
     )
     margins = exchange(margins, "feat")
-    parts, loss = kernel_call(
-        functools.partial(grad_kernel, float(tokens * rows), share),
-        (shape(rows, share // 2 + kinds, 2, LANES), shape(tokens // LANES, LANES)),
-        (margins, wins, gap, pick, proj, held),
-        "grads",
+    half = shape(chips, share // 2, 2, LANES)
+    other, loss, left, weighted = kernel_call(
+        functools.partial(other_kernel, float(tokens * rows)),
+        (
+            half,
+            shape(tokens // LANES, LANES),
+            pltpu.VMEM((R + 2 * NM, tokens), BF16),
+            pltpu.VMEM((NM, width // 2), F32),
+        ),
+        (margins, wins, gap, pick, held),
         24,
-        (4 * tokens * width * R, tokens * width * 2),
-        scratch=[pltpu.VMEM((tokens // LANES, LANES), F32), pltpu.VMEM((R + 2 * NM, width), F32)],
-    )
-    parts = exchange(parts, ROWS)
+        (2 * tokens * width * R, tokens * width * 2),
+        scratch=[pltpu.VMEM((tokens // LANES, LANES), F32), pltpu.VMEM((R + 2 * NM, width // 2), F32)],
+    )
+    other = swap(other)
+    own, model_grad = kernel_call(
+        own_kernel,
+        (half, shape(chips, kinds // 2, 2, LANES)),
+        (left, weighted, proj, held),
+        24,
+        (2 * tokens * width * R, tokens * width * 2),
+    )
+    parts = kernel_call(
+        join_kernel, shape(chips, (share + kinds) // 2, 2, LANES), (own, other, model_grad), 4, (10000, 400000)
+    )
+    parts = exchange(parts, CHIPS)
     grad_share, parts = kernel_call(
-        share_kernel,
-        (shape(share // 2, 2, LANES), shape(feats, kinds + 1, 2, LANES)),
-        (parts,),
-        "shares",
+        functools.partial(share_kernel, float(feats)),
+        (shape(share // 2, 2, LANES), shape(2 * feats, kinds // 2 + 1, 2, LANES)),
+        (parts, loss),
         4,
         (10000, 400000),
     )
-    parts = exchange(parts, "feat")
+    other_share = swap(grad_share)
+    parts = exchange(parts, (CORE, "feat"))
+    parts = kernel_call(sum_kernel, shape(*parts.shape[1:]), (parts,), 4, (10000, 100000))
+    length = 2 * share + kinds + 2
     parts = kernel_call(
-        pack_kernel,
-        shape(rows, share // 2 + kinds + 1, 2, LANES),
-        (parts, grad_share, loss),
-        "pack",
-        4,
-        (10000, 400000),
-    )
-    parts = exchange(parts, ROWS)
+        pack_kernel, shape(chips, length + -length % 8, LANES), (parts, grad_share, other_share), 4, (10000, 400000)
+    )
+    parts = exchange(parts, CHIPS)
     update_proj, update_models, loss = kernel_call(
-        functools.partial(final_kernel, share),
+        functools.partial(final_kernel, share, kinds),
         (shape(width, R), shape(NM, R), shape(1, 1)),
         (parts,),
-        "final",
         4,
         (10000, 600000),
     )

time: 68.2 us -> 66.4 us (0.974)
  blocking collectives: 59.6 us -> 42.1 us
  starting transfers between devices: 0 us -> 7.89 us
  waiting for transfers between devices: 0 us -> 6.78 us
  Pallas kernels: 7.67 us -> 8.71 us
    all_to_all x4 -> x3, blocking collectives: 59.6 us -> 42.1 us  [exchange(): return lax.all_to_all(x, axis, split_axis=0, concat_axis=0, tiled=True)]
    all_to_all x0 -> x1, waiting for transfers between devices: none -> 6.77 us  [exchange(): return lax.all_to_all(x, axis, split_axis=0, concat_axis=0, tiled=True)]
    all_to_all x0 -> x1, starting transfers between devices: none -> 4.98 us  [exchange(): return lax.all_to_all(x, axis, split_axis=0, concat_axis=0, tiled=True)]
    ppermute x0 -> x2, starting transfers between devices: none -> 2.9 us  [swap(): return lax.ppermute(x, CORE, [(0, 1), (1, 0)])]
    pallas_call x5 -> x8, Pallas kernels: 7.67 us -> 8.71 us  [kernel_call(): pl.pallas_call(body, out_shape=outs, in_specs=in_specs or [VMEM] * len(in...]
  transfers between devices with their start and end apart: 0 -> 3, of which waited for: 0 -> 1; matrix products, arithmetic and copies ran while one was open for 0% -> 0% of each run, Pallas kernels for 0% -> 2%
where the time goes in v5:
time: 66.4 us; the launch traced here: 66.1 us
  blocking collectives  42.1 us (63%)
  Pallas kernels  8.71 us (13%)
  starting transfers between devices  7.89 us (12%)
  waiting for transfers between devices  6.78 us (10%)
  between operations  0.7 us (1%)
    all_to_all x3, blocking collectives, exchange(): return lax.all_to_all(x, axis, split_axis=0, concat_axis=0, tiled=True)  42.1 us
    pallas_call x8, Pallas kernels, kernel_call(): pl.pallas_call(body, out_shape=outs, in_specs=in_specs or [VMEM] * len(in...  8.71 us
    all_to_all x1, waiting for transfers between devices, exchange(): return lax.all_to_all(x, axis, split_axis=0, concat_axis=0, tiled=True)  6.77 us
    all_to_all x1, starting transfers between devices, exchange(): return lax.all_to_all(x, axis, split_axis=0, concat_axis=0, tiled=True)  4.98 us
    ppermute x2, starting transfers between devices, swap(): return lax.ppermute(x, CORE, [(0, 1), (1, 0)])  2.9 us
  transfers between devices with their start and end apart: 3, of which 1 were waited for; matrix products, arithmetic and copies ran while one was open for 0% of the time, Pallas kernels for 2%

profile of v5, /device:TPU:1, one launch (start us, length us, event | category | flops | bytes accessed | tf_op | source)
XLA Modules:
  0.0 66.1 jit_solution(14063516711545478933)
XLA Ops:
  0.6 0.0 copy-start
  0.6 4.6 %shard_map.85 = (f32[8,48,128]{2,1,0:T(8,128)S(1)}, bf16[6144,512]{1,0:T(8,128)(2,1)S(1)}, f32[128,6144]{1,0:T(8,128)S(1)}, bf16[64,6144]{1,0:T(8,128)(2,1)S(1)}, bf16[512,128]{1,0:T(8,128)(2,1)S(1)}) custom-call(s32[48,128]{1,0:T(8,128)} %bitcast.5, s32[48,128]{1,0:T(8,128)} %bitcast.6, f32[64,128]{1,0:T(8,128)} %models_hbm.1, bf16[512,128]{1,0:T(8,128)(2,1)} %proj_hbm.1, ...), custom_call_target="tpu_custom_call" | custom-call | flops 805306368 | bytes 6291456 | tf_op jit(solution)/shard_map/pallas_call | solution.py:225
  5.3 17.8 %all_to_all.20.margins_ref = f32[8,48,128]{2,1,0:T(8,128)S(1)} all-to-all(f32[8,48,128]{2,1,0:T(8,128)S(1)} %get-tuple-element.19), channel_id=1, replica_groups=mesh['rows_0'=4,'rows_1'=4,'rows_2'=2,'feat'=8] {'feat'}, dimensions={0} | all-to-all | bytes 393216 | tf_op jit(solution)/shard_map/all_to_all | solution.py:28
  23.1 0.0 copy-done
  23.1 1.2 %shard_map.86 = (f32[16,8,2,128]{3,2,1,0:T(2,128)S(1)}, f32[48,128]{1,0:T(8,128)S(1)}, bf16[256,6144]{1,0:T(8,128)(2,1)S(1)}, f32[64,256]{1,0:T(8,128)S(1)}) custom-call(f32[8,48,128]{2,1,0:T(8,128)S(1)} %all_to_all.20.margins_ref, s32[48,128]{1,0:T(8,128)S(1)} %bitcast.4, f32[128,6144]{1,0:T(8,128)S(1)} %get-tuple-element.20.gap_ref, ...), custom_call_target="tpu_custom_call" | custom-call | flops 805306368 | bytes 6291456 | tf_op jit(solution)/shard_map/pallas_call | solution.py:225
  24.2 2.6 %collective-permute-start = (f32[16,8,2,128]{3,2,1,0:T(2,128)S(1)}, f32[16,8,2,128]{3,2,1,0:T(2,128)S(1)}, u32[]{:S(2)}, u32[]{:S(2)}) collective-permute-start(f32[16,8,2,128]{3,2,1,0:T(2,128)S(1)} %get-tuple-element.27), channel_id=1, source_target_pairs={{0,8},{8,0},{1,9},{9,1},{2,10},{10,2},{3,11},{11,3},{4,12},{12,4},... | collective-permute-start | bytes 393224 | tf_op jit(solution)/shard_map/ppermute | solution.py:32
  26.9 1.3 %shard_map.87 = (f32[16,8,2,128]{3,2,1,0:T(2,128)S(1)}, f32[16,2,2,128]{3,2,1,0:T(2,128)S(1)}) custom-call(bf16[256,6144]{1,0:T(8,128)(2,1)S(1)} %get-tuple-element.23.left_ref, f32[64,256]{1,0:T(8,128)S(1)} %get-tuple-element.24.weighted_ref, bf16[512,128]{1,0:T(8,128)(2,1)S(1)} %get-tuple-element.25.proj_ref, bf16[6144,512]{1,0:T(8,128)(2,1)S(1)} %get-tuple-element.22.q_ref), custom_call_target="tpu_custom_call" | custom-call | flops 805306368 | bytes 6291456 | tf_op jit(solution)/shard_map/pallas_call | solution.py:225
  28.2 0.0 collective-permute-done.other_ref
  28.2 0.1 shard_map.88
  28.3 13.4 %all_to_all.21.parts_ref = f32[16,10,2,128]{3,2,1,0:T(2,128)S(1)} all-to-all(f32[16,10,2,128]{3,2,1,0:T(2,128)S(1)} %shard_map.88), channel_id=1, replica_groups=mesh['rows_0'=4,'rows_1'=4,'rows_2'=2,'feat'=8] {'rows_0','rows_1'}, dimensions={0} | all-to-all | bytes 327680 | tf_op jit(solution)/shard_map/all_to_all | solution.py:28
  41.7 0.7 %shard_map.89 = (f32[8,2,128]{2,1,0:T(2,128)S(1)}, f32[16,3,2,128]{3,2,1,0:T(2,128)}) custom-call(f32[16,10,2,128]{3,2,1,0:T(2,128)S(1)} %all_to_all.21.parts_ref, f32[48,128]{1,0:T(8,128)S(1)} %get-tuple-element.29.loss_ref), custom_call_target="tpu_custom_call" | custom-call | flops 10000 | bytes 400000 | tf_op jit(solution)/shard_map/pallas_call | solution.py:225
  42.3 5.0 %all-to-all-start.2 = ((f32[16,3,2,128]{3,2,1,0:T(2,128)}), f32[16,3,2,128]{3,2,1,0:T(2,128)S(1)}, u32[]{:S(2)}, u32[]{:S(2)}) async-start(f32[16,3,2,128]{3,2,1,0:T(2,128)} %get-tuple-element.30), calls=%async_computation.2 | async-start | bytes 98304 | tf_op jit(solution)/shard_map/all_to_all | solution.py:28
  47.3 0.3 collective-permute-start.1
  47.6 6.8 %all-to-all-done.2.parts_ref = f32[16,3,2,128]{3,2,1,0:T(2,128)S(1)} async-done(((f32[16,3,2,128]{3,2,1,0:T(2,128)}), f32[16,3,2,128]{3,2,1,0:T(2,128)S(1)}, u32[]{:S(2)}, u32[]{:S(2)}) %all-to-all-start.2) | async-done | bytes 49184 | tf_op jit(solution)/shard_map/all_to_all | solution.py:28
  54.4 0.0 collective-permute-done.1.other_ref
  54.4 10.9 %all_to_all.22.parts_ref = f32[16,40,128]{2,1,0:T(8,128)S(1)} all-to-all(f32[16,40,128]{2,1,0:T(8,128)S(1)} %shard_map.91), channel_id=1, replica_groups=mesh['rows_0'=4,'rows_1'=4,'rows_2'=2,'feat'=8] {'rows_0','rows_1'}, dimensions={0} | all-to-all | bytes 655360 | tf_op jit(solution)/shard_map/all_to_all | solution.py:28
  65.3 0.8 %shard_map.92 = (f32[512,128]{1,0:T(8,128)}, f32[64,128]{1,0:T(8,128)}, f32[1,1]{1,0:T(1,128)}) custom-call(f32[16,40,128]{2,1,0:T(8,128)S(1)} %all_to_all.22.parts_ref), custom_call_target="tpu_custom_call" | custom-call | flops 10000 | bytes 600000 | tf_op jit(solution)/shard_map/pallas_call | solution.py:225
  (2 shorter events, 0.1 us)
Async XLA Ops:
  0.6 22.4 %copy-start = (s32[6144]{0:T(1024)S(1)}, s32[6144]{0:T(1024)}, u32[]{:S(2)}) copy-start(s32[6144]{0:T(1024)} %param.11) | copy-start | bytes 73732
  24.2 3.9 %collective-permute-start = (f32[16,8,2,128]{3,2,1,0:T(2,128)S(1)}, f32[16,8,2,128]{3,2,1,0:T(2,128)S(1)}, u32[]{:S(2)}, u32[]{:S(2)}) collective-permute-start(f32[16,8,2,128]{3,2,1,0:T(2,128)S(1)} %get-tuple-element.27), channel_id=1, source_target_pairs={{0,8},{8,0},{1,9},{9,1},{2,10},{10,2},{3,11},{11,3},{4,12},{12,4},... | collective-permute-start | bytes 393224 | tf_op jit(solution)/shard_map/ppermute | solution.py:32
  42.3 12.0 %all-to-all-start.2 = ((f32[16,3,2,128]{3,2,1,0:T(2,128)}), f32[16,3,2,128]{3,2,1,0:T(2,128)S(1)}, u32[]{:S(2)}, u32[]{:S(2)}) async-start(f32[16,3,2,128]{3,2,1,0:T(2,128)} %get-tuple-element.30), calls=%async_computation.2 | async-start | bytes 98304 | tf_op jit(solution)/shard_map/all_to_all | solution.py:28
  47.3 7.1 %collective-permute-start.1 = (f32[8,2,128]{2,1,0:T(2,128)S(1)}, f32[8,2,128]{2,1,0:T(2,128)S(1)}, u32[]{:S(2)}, u32[]{:S(2)}) collective-permute-start(f32[8,2,128]{2,1,0:T(2,128)S(1)} %get-tuple-element.31.own_ref), channel_id=1, source_target_pairs={{0,8},{8,0},{1,9},{9,1},{2,10},{10,2},{3,11},{11,3},{4,12},{12,4},... | collective-permute-start | bytes 24584 | tf_op jit(solution)/shard_map/ppermute | solution.py:32

commit v6 on v5

--- a/solution.py
+++ b/solution.py
@@ -19,9 +19,8 @@
 F32 = jnp.float32
 BF16 = jnp.bfloat16
 MIB = 1 << 20
-BLOCK = 1024
+BLOCK = 1536
 AHEAD = 2
-CHUNK = 2048
 
 
 def exchange(x, axis):
@@ -84,12 +83,11 @@
             started += 1
     small[3].wait()
     proj = proj_ref[...].astype(F32).T.astype(BF16)
-    for start in range(0, tokens, CHUNK):
-        for i in range(start // BLOCK, (start + CHUNK) // BLOCK):
-            copies[i].wait()
-        routed = contract(proj, q_ref[start : start + CHUNK, :], 1, 1)
-        margin = jnp.sum(routed * gap_ref[:, start : start + CHUNK], axis=0, keepdims=True)
-        for j in range(CHUNK // LANES):
+    for start in range(0, tokens, BLOCK):
+        copies[start // BLOCK].wait()
+        routed = contract(proj, q_ref[start : start + BLOCK, :], 1, 1)
+        margin = jnp.sum(routed * gap_ref[:, start : start + BLOCK], axis=0, keepdims=True)
+        for j in range(BLOCK // LANES):
             row = margin[:, j * LANES : (j + 1) * LANES]
             for k in range(out_ref.shape[0]):
                 out_ref[k, start // LANES + j : start // LANES + j + 1, :] = row
@@ -108,7 +106,7 @@
     return pl.ds(pl.multiple_of(half * width, width), width)
 
 
-def other_kernel(total, margins_ref, wins_ref, gap_ref, pick_ref, q_ref, out_ref, loss_ref, left_ref, weighted_ref, coef_ref, acc_ref):
+def other_kernel(total, margins_ref, wins_ref, gap_ref, pick_ref, q_ref, out_ref, wrong_ref, left_ref, weighted_ref, coef_ref, acc_ref):
     tokens = q_ref.shape[0]
     width = acc_ref.shape[1]
     margin = margins_ref[0]
@@ -116,7 +114,7 @@
         margin = margin + margins_ref[k]
     sign = 2.0 * wins_ref[...].astype(F32) - 1.0
     wrong = -sign * margin
-    loss_ref[...] = jax.nn.softplus(wrong) / total
+    wrong_ref[...] = wrong
     coef_ref[...] = -sign * jax.nn.sigmoid(wrong) / total
     other = columns(1 - lax.axis_index(CORE), width)
     for start in range(0, tokens, BLOCK):
@@ -135,7 +133,8 @@
     weighted_ref[...] = acc_ref[R : R + NM, :] + acc_ref[R + NM :, :]
 
 
-def own_kernel(left_ref, weighted_ref, proj_ref, q_ref, out_ref, models_ref):
+def own_kernel(total, left_ref, weighted_ref, wrong_ref, proj_ref, q_ref, out_ref, models_ref, loss_ref):
+    loss_ref[...] = jax.nn.softplus(wrong_ref[...]) / total
     width = weighted_ref.shape[1]
     core = lax.axis_index(CORE)
     acc = contract(left_ref[...], q_ref[:, columns(core, width)], 1, 0)
@@ -267,7 +266,7 @@
     )
     margins = exchange(margins, "feat")
     half = shape(chips, share // 2, 2, LANES)
-    other, loss, left, weighted = kernel_call(
+    other, wrong, left, weighted = kernel_call(
         functools.partial(other_kernel, float(tokens * rows)),
         (
             half,
@@ -281,10 +280,10 @@
         scratch=[pltpu.VMEM((tokens // LANES, LANES), F32), pltpu.VMEM((R + 2 * NM, width // 2), F32)],
     )
     other = swap(other)
-    own, model_grad = kernel_call(
-        own_kernel,
-        (half, shape(chips, kinds // 2, 2, LANES)),
-        (left, weighted, proj, held),
+    own, model_grad, loss = kernel_call(
+        functools.partial(own_kernel, float(tokens * rows)),
+        (half, shape(chips, kinds // 2, 2, LANES), shape(tokens // LANES, LANES)),
+        (left, weighted, wrong, proj, held),
         24,
         (2 * tokens * width * R, tokens * width * 2),
     )

time: 66.4 us -> 66.1 us (level)
  no operation moved by 1% of the time
where the time goes in v6:
time: 66.1 us; the launch traced here: 65.8 us
  blocking collectives  42.1 us (64%)
  Pallas kernels  8.37 us (13%)
  starting transfers between devices  7.86 us (12%)
  waiting for transfers between devices  6.78 us (10%)
  between operations  0.7 us (1%)
    all_to_all x3, blocking collectives, exchange(): return lax.all_to_all(x, axis, split_axis=0, concat_axis=0, tiled=True)  42.1 us
    pallas_call x8, Pallas kernels, kernel_call(): pl.pallas_call(body, out_shape=outs, in_specs=in_specs or [VMEM] * len(in...  8.37 us
    all_to_all x1, waiting for transfers between devices, exchange(): return lax.all_to_all(x, axis, split_axis=0, concat_axis=0, tiled=True)  6.77 us
    all_to_all x1, starting transfers between devices, exchange(): return lax.all_to_all(x, axis, split_axis=0, concat_axis=0, tiled=True)  4.96 us
    ppermute x2, starting transfers between devices, swap(): return lax.ppermute(x, CORE, [(0, 1), (1, 0)])  2.9 us
  transfers between devices with their start and end apart: 3, of which 1 were waited for; matrix products, arithmetic and copies ran while one was open for 0% of the time, Pallas kernels for 2%

profile of v6, /device:TPU:1, one launch (start us, length us, event | category | flops | bytes accessed | tf_op | source)
XLA Modules:
  0.0 65.8 jit_solution(12807919415400880596)
XLA Ops:
  0.6 0.0 copy-start
  0.6 4.2 %shard_map.85 = (f32[8,48,128]{2,1,0:T(8,128)S(1)}, bf16[6144,512]{1,0:T(8,128)(2,1)S(1)}, f32[128,6144]{1,0:T(8,128)S(1)}, bf16[64,6144]{1,0:T(8,128)(2,1)S(1)}, bf16[512,128]{1,0:T(8,128)(2,1)S(1)}) custom-call(s32[48,128]{1,0:T(8,128)} %bitcast.5, s32[48,128]{1,0:T(8,128)} %bitcast.6, f32[64,128]{1,0:T(8,128)} %models_hbm.1, bf16[512,128]{1,0:T(8,128)(2,1)} %proj_hbm.1, ...), custom_call_target="tpu_custom_call" | custom-call | flops 805306368 | bytes 6291456 | tf_op jit(solution)/shard_map/pallas_call | solution.py:224
  4.9 17.8 %all_to_all.20.margins_ref = f32[8,48,128]{2,1,0:T(8,128)S(1)} all-to-all(f32[8,48,128]{2,1,0:T(8,128)S(1)} %get-tuple-element.20), channel_id=1, replica_groups=mesh['rows_0'=4,'rows_1'=4,'rows_2'=2,'feat'=8] {'feat'}, dimensions={0} | all-to-all | bytes 393216 | tf_op jit(solution)/shard_map/all_to_all | solution.py:27
  22.7 0.0 copy-done
  22.7 1.2 %shard_map.86 = (f32[16,8,2,128]{3,2,1,0:T(2,128)S(1)}, f32[48,128]{1,0:T(8,128)S(1)}, bf16[256,6144]{1,0:T(8,128)(2,1)S(1)}, f32[64,256]{1,0:T(8,128)S(1)}) custom-call(f32[8,48,128]{2,1,0:T(8,128)S(1)} %all_to_all.20.margins_ref, s32[48,128]{1,0:T(8,128)S(1)} %bitcast.4, f32[128,6144]{1,0:T(8,128)S(1)} %get-tuple-element.21.gap_ref, ...), custom_call_target="tpu_custom_call" | custom-call | flops 805306368 | bytes 6291456 | tf_op jit(solution)/shard_map/pallas_call | solution.py:224
  23.9 2.6 %collective-permute-start = (f32[16,8,2,128]{3,2,1,0:T(2,128)S(1)}, f32[16,8,2,128]{3,2,1,0:T(2,128)S(1)}, u32[]{:S(2)}, u32[]{:S(2)}) collective-permute-start(f32[16,8,2,128]{3,2,1,0:T(2,128)S(1)} %get-tuple-element.29), channel_id=1, source_target_pairs={{0,8},{8,0},{1,9},{9,1},{2,10},{10,2},{3,11},{11,3},{4,12},{12,4},... | collective-permute-start | bytes 393224 | tf_op jit(solution)/shard_map/ppermute | solution.py:31
  26.5 1.3 %shard_map.87 = (f32[16,8,2,128]{3,2,1,0:T(2,128)S(1)}, f32[16,2,2,128]{3,2,1,0:T(2,128)S(1)}, f32[48,128]{1,0:T(8,128)S(1)}) custom-call(bf16[256,6144]{1,0:T(8,128)(2,1)S(1)} %get-tuple-element.24.left_ref, f32[64,256]{1,0:T(8,128)S(1)} %get-tuple-element.25.weighted_ref, f32[48,128]{1,0:T(8,128)S(1)} %get-tuple-element.26.wrong_ref, ...), custom_call_target="tpu_custom_call" | custom-call | flops 805306368 | bytes 6291456 | tf_op jit(solution)/shard_map/pallas_call | solution.py:224
  27.8 0.0 collective-permute-done.other_ref
  27.8 0.1 shard_map.88
  27.9 13.4 %all_to_all.21.parts_ref = f32[16,10,2,128]{3,2,1,0:T(2,128)S(1)} all-to-all(f32[16,10,2,128]{3,2,1,0:T(2,128)S(1)} %shard_map.88), channel_id=1, replica_groups=mesh['rows_0'=4,'rows_1'=4,'rows_2'=2,'feat'=8] {'rows_0','rows_1'}, dimensions={0} | all-to-all | bytes 327680 | tf_op jit(solution)/shard_map/all_to_all | solution.py:27
  41.3 0.7 %shard_map.89 = (f32[8,2,128]{2,1,0:T(2,128)S(1)}, f32[16,3,2,128]{3,2,1,0:T(2,128)}) custom-call(f32[16,10,2,128]{3,2,1,0:T(2,128)S(1)} %all_to_all.21.parts_ref, f32[48,128]{1,0:T(8,128)S(1)} %get-tuple-element.31.loss_ref), custom_call_target="tpu_custom_call" | custom-call | flops 10000 | bytes 400000 | tf_op jit(solution)/shard_map/pallas_call | solution.py:224
  42.0 5.0 %all-to-all-start.2 = ((f32[16,3,2,128]{3,2,1,0:T(2,128)}), f32[16,3,2,128]{3,2,1,0:T(2,128)S(1)}, u32[]{:S(2)}, u32[]{:S(2)}) async-start(f32[16,3,2,128]{3,2,1,0:T(2,128)} %get-tuple-element.32), calls=%async_computation.2 | async-start | bytes 98304 | tf_op jit(solution)/shard_map/all_to_all | solution.py:27
  47.0 0.3 collective-permute-start.1
  47.2 6.8 %all-to-all-done.2.parts_ref = f32[16,3,2,128]{3,2,1,0:T(2,128)S(1)} async-done(((f32[16,3,2,128]{3,2,1,0:T(2,128)}), f32[16,3,2,128]{3,2,1,0:T(2,128)S(1)}, u32[]{:S(2)}, u32[]{:S(2)}) %all-to-all-start.2) | async-done | bytes 49184 | tf_op jit(solution)/shard_map/all_to_all | solution.py:27
  54.0 0.0 collective-permute-done.1.other_ref
  54.1 10.9 %all_to_all.22.parts_ref = f32[16,40,128]{2,1,0:T(8,128)S(1)} all-to-all(f32[16,40,128]{2,1,0:T(8,128)S(1)} %shard_map.91), channel_id=1, replica_groups=mesh['rows_0'=4,'rows_1'=4,'rows_2'=2,'feat'=8] {'rows_0','rows_1'}, dimensions={0} | all-to-all | bytes 655360 | tf_op jit(solution)/shard_map/all_to_all | solution.py:27
  65.0 0.8 %shard_map.92 = (f32[512,128]{1,0:T(8,128)}, f32[64,128]{1,0:T(8,128)}, f32[1,1]{1,0:T(1,128)}) custom-call(f32[16,40,128]{2,1,0:T(8,128)S(1)} %all_to_all.22.parts_ref), custom_call_target="tpu_custom_call" | custom-call | flops 10000 | bytes 600000 | tf_op jit(solution)/shard_map/pallas_call | solution.py:224
  (2 shorter events, 0.1 us)
Async XLA Ops:
  0.6 22.1 %copy-start = (s32[6144]{0:T(1024)S(1)}, s32[6144]{0:T(1024)}, u32[]{:S(2)}) copy-start(s32[6144]{0:T(1024)} %param.11) | copy-start | bytes 73732
  23.9 3.9 %collective-permute-start = (f32[16,8,2,128]{3,2,1,0:T(2,128)S(1)}, f32[16,8,2,128]{3,2,1,0:T(2,128)S(1)}, u32[]{:S(2)}, u32[]{:S(2)}) collective-permute-start(f32[16,8,2,128]{3,2,1,0:T(2,128)S(1)} %get-tuple-element.29), channel_id=1, source_target_pairs={{0,8},{8,0},{1,9},{9,1},{2,10},{10,2},{3,11},{11,3},{4,12},{12,4},... | collective-permute-start | bytes 393224 | tf_op jit(solution)/shard_map/ppermute | solution.py:31
  42.0 12.0 %all-to-all-start.2 = ((f32[16,3,2,128]{3,2,1,0:T(2,128)}), f32[16,3,2,128]{3,2,1,0:T(2,128)S(1)}, u32[]{:S(2)}, u32[]{:S(2)}) async-start(f32[16,3,2,128]{3,2,1,0:T(2,128)} %get-tuple-element.32), calls=%async_computation.2 | async-start | bytes 98304 | tf_op jit(solution)/shard_map/all_to_all | solution.py:27
  47.0 7.1 %collective-permute-start.1 = (f32[8,2,128]{2,1,0:T(2,128)S(1)}, f32[8,2,128]{2,1,0:T(2,128)S(1)}, u32[]{:S(2)}, u32[]{:S(2)}) collective-permute-start(f32[8,2,128]{2,1,0:T(2,128)S(1)} %get-tuple-element.33.own_ref), channel_id=1, source_target_pairs={{0,8},{8,0},{1,9},{9,1},{2,10},{10,2},{3,11},{11,3},{4,12},{12,4},... | collective-permute-start | bytes 24584 | tf_op jit(solution)/shard_map/ppermute | solution.py:31

commit v7 on v6

--- a/solution.py
+++ b/solution.py
@@ -21,6 +21,7 @@
 MIB = 1 << 20
 BLOCK = 1536
 AHEAD = 2
+GAPS = 3072
 
 
 def exchange(x, axis):
@@ -73,14 +74,16 @@
         copy.wait()
     table = model_table(models_ref[...])
     started = AHEAD
-    for start in range(0, tokens, BLOCK):
-        cut = slice(start, start + BLOCK)
-        pick = picks(first_ref, second_ref, start, BLOCK).astype(BF16)
+    for start in range(0, tokens, GAPS):
+        cut = slice(start, start + GAPS)
+        pick = picks(first_ref, second_ref, start, GAPS).astype(BF16)
         pick_ref[:, cut] = pick
         gap_ref[:, cut] = contract(table, jnp.concatenate([pick, pick, pick], axis=0), 1, 0)
-        if start > 0 and started < len(copies):
+        if started < len(copies):
             copies[started].start()
             started += 1
+    for copy in copies[started:]:
+        copy.start()
     small[3].wait()
     proj = proj_ref[...].astype(F32).T.astype(BF16)
     for start in range(0, tokens, BLOCK):

time: 66.1 us -> 66.1 us (level)
  no operation moved by 1% of the time
where the time goes in v7:
time: 66.1 us; the launch traced here: 65.8 us
  blocking collectives  42.1 us (64%)
  Pallas kernels  8.37 us (13%)
  starting transfers between devices  7.86 us (12%)
  waiting for transfers between devices  6.78 us (10%)
  between operations  0.7 us (1%)
    all_to_all x3, blocking collectives, exchange(): return lax.all_to_all(x, axis, split_axis=0, concat_axis=0, tiled=True)  42.1 us
    pallas_call x8, Pallas kernels, kernel_call(): pl.pallas_call(body, out_shape=outs, in_specs=in_specs or [VMEM] * len(in...  8.37 us
    all_to_all x1, waiting for transfers between devices, exchange(): return lax.all_to_all(x, axis, split_axis=0, concat_axis=0, tiled=True)  6.77 us
    all_to_all x1, starting transfers between devices, exchange(): return lax.all_to_all(x, axis, split_axis=0, concat_axis=0, tiled=True)  4.96 us
    ppermute x2, starting transfers between devices, swap(): return lax.ppermute(x, CORE, [(0, 1), (1, 0)])  2.9 us
  transfers between devices with their start and end apart: 3, of which 1 were waited for; matrix products, arithmetic and copies ran while one was open for 0% of the time, Pallas kernels for 2%

profile of v7, /device:TPU:1, one launch (start us, length us, event | category | flops | bytes accessed | tf_op | source)
XLA Modules:
  0.0 65.8 jit_solution(12807919415400880596)
XLA Ops:
  0.6 0.0 copy-start
  0.6 4.2 %shard_map.85 = (f32[8,48,128]{2,1,0:T(8,128)S(1)}, bf16[6144,512]{1,0:T(8,128)(2,1)S(1)}, f32[128,6144]{1,0:T(8,128)S(1)}, bf16[64,6144]{1,0:T(8,128)(2,1)S(1)}, bf16[512,128]{1,0:T(8,128)(2,1)S(1)}) custom-call(s32[48,128]{1,0:T(8,128)} %bitcast.5, s32[48,128]{1,0:T(8,128)} %bitcast.6, f32[64,128]{1,0:T(8,128)} %models_hbm.1, bf16[512,128]{1,0:T(8,128)(2,1)} %proj_hbm.1, ...), custom_call_target="tpu_custom_call" | custom-call | flops 805306368 | bytes 6291456 | tf_op jit(solution)/shard_map/pallas_call | solution.py:227
  4.9 17.8 %all_to_all.20.margins_ref = f32[8,48,128]{2,1,0:T(8,128)S(1)} all-to-all(f32[8,48,128]{2,1,0:T(8,128)S(1)} %get-tuple-element.20), channel_id=1, replica_groups=mesh['rows_0'=4,'rows_1'=4,'rows_2'=2,'feat'=8] {'feat'}, dimensions={0} | all-to-all | bytes 393216 | tf_op jit(solution)/shard_map/all_to_all | solution.py:28
  22.7 0.0 copy-done
  22.7 1.2 %shard_map.86 = (f32[16,8,2,128]{3,2,1,0:T(2,128)S(1)}, f32[48,128]{1,0:T(8,128)S(1)}, bf16[256,6144]{1,0:T(8,128)(2,1)S(1)}, f32[64,256]{1,0:T(8,128)S(1)}) custom-call(f32[8,48,128]{2,1,0:T(8,128)S(1)} %all_to_all.20.margins_ref, s32[48,128]{1,0:T(8,128)S(1)} %bitcast.4, f32[128,6144]{1,0:T(8,128)S(1)} %get-tuple-element.21.gap_ref, ...), custom_call_target="tpu_custom_call" | custom-call | flops 805306368 | bytes 6291456 | tf_op jit(solution)/shard_map/pallas_call | solution.py:227
  23.9 2.6 %collective-permute-start = (f32[16,8,2,128]{3,2,1,0:T(2,128)S(1)}, f32[16,8,2,128]{3,2,1,0:T(2,128)S(1)}, u32[]{:S(2)}, u32[]{:S(2)}) collective-permute-start(f32[16,8,2,128]{3,2,1,0:T(2,128)S(1)} %get-tuple-element.29), channel_id=1, source_target_pairs={{0,8},{8,0},{1,9},{9,1},{2,10},{10,2},{3,11},{11,3},{4,12},{12,4},... | collective-permute-start | bytes 393224 | tf_op jit(solution)/shard_map/ppermute | solution.py:32
  26.5 1.3 %shard_map.87 = (f32[16,8,2,128]{3,2,1,0:T(2,128)S(1)}, f32[16,2,2,128]{3,2,1,0:T(2,128)S(1)}, f32[48,128]{1,0:T(8,128)S(1)}) custom-call(bf16[256,6144]{1,0:T(8,128)(2,1)S(1)} %get-tuple-element.24.left_ref, f32[64,256]{1,0:T(8,128)S(1)} %get-tuple-element.25.weighted_ref, f32[48,128]{1,0:T(8,128)S(1)} %get-tuple-element.26.wrong_ref, ...), custom_call_target="tpu_custom_call" | custom-call | flops 805306368 | bytes 6291456 | tf_op jit(solution)/shard_map/pallas_call | solution.py:227
  27.8 0.0 collective-permute-done.other_ref
  27.8 0.1 shard_map.88
  27.9 13.4 %all_to_all.21.parts_ref = f32[16,10,2,128]{3,2,1,0:T(2,128)S(1)} all-to-all(f32[16,10,2,128]{3,2,1,0:T(2,128)S(1)} %shard_map.88), channel_id=1, replica_groups=mesh['rows_0'=4,'rows_1'=4,'rows_2'=2,'feat'=8] {'rows_0','rows_1'}, dimensions={0} | all-to-all | bytes 327680 | tf_op jit(solution)/shard_map/all_to_all | solution.py:28
  41.3 0.7 %shard_map.89 = (f32[8,2,128]{2,1,0:T(2,128)S(1)}, f32[16,3,2,128]{3,2,1,0:T(2,128)}) custom-call(f32[16,10,2,128]{3,2,1,0:T(2,128)S(1)} %all_to_all.21.parts_ref, f32[48,128]{1,0:T(8,128)S(1)} %get-tuple-element.31.loss_ref), custom_call_target="tpu_custom_call" | custom-call | flops 10000 | bytes 400000 | tf_op jit(solution)/shard_map/pallas_call | solution.py:227
  42.0 5.0 %all-to-all-start.2 = ((f32[16,3,2,128]{3,2,1,0:T(2,128)}), f32[16,3,2,128]{3,2,1,0:T(2,128)S(1)}, u32[]{:S(2)}, u32[]{:S(2)}) async-start(f32[16,3,2,128]{3,2,1,0:T(2,128)} %get-tuple-element.32), calls=%async_computation.2 | async-start | bytes 98304 | tf_op jit(solution)/shard_map/all_to_all | solution.py:28
  47.0 0.3 collective-permute-start.1
  47.2 6.8 %all-to-all-done.2.parts_ref = f32[16,3,2,128]{3,2,1,0:T(2,128)S(1)} async-done(((f32[16,3,2,128]{3,2,1,0:T(2,128)}), f32[16,3,2,128]{3,2,1,0:T(2,128)S(1)}, u32[]{:S(2)}, u32[]{:S(2)}) %all-to-all-start.2) | async-done | bytes 49184 | tf_op jit(solution)/shard_map/all_to_all | solution.py:28
  54.0 0.0 collective-permute-done.1.other_ref
  54.1 10.9 %all_to_all.22.parts_ref = f32[16,40,128]{2,1,0:T(8,128)S(1)} all-to-all(f32[16,40,128]{2,1,0:T(8,128)S(1)} %shard_map.91), channel_id=1, replica_groups=mesh['rows_0'=4,'rows_1'=4,'rows_2'=2,'feat'=8] {'rows_0','rows_1'}, dimensions={0} | all-to-all | bytes 655360 | tf_op jit(solution)/shard_map/all_to_all | solution.py:28
  65.0 0.8 %shard_map.92 = (f32[512,128]{1,0:T(8,128)}, f32[64,128]{1,0:T(8,128)}, f32[1,1]{1,0:T(1,128)}) custom-call(f32[16,40,128]{2,1,0:T(8,128)S(1)} %all_to_all.22.parts_ref), custom_call_target="tpu_custom_call" | custom-call | flops 10000 | bytes 600000 | tf_op jit(solution)/shard_map/pallas_call | solution.py:227
  (2 shorter events, 0.1 us)
Async XLA Ops:
  0.6 22.1 %copy-start = (s32[6144]{0:T(1024)S(1)}, s32[6144]{0:T(1024)}, u32[]{:S(2)}) copy-start(s32[6144]{0:T(1024)} %param.11) | copy-start | bytes 73732
  23.9 3.9 %collective-permute-start = (f32[16,8,2,128]{3,2,1,0:T(2,128)S(1)}, f32[16,8,2,128]{3,2,1,0:T(2,128)S(1)}, u32[]{:S(2)}, u32[]{:S(2)}) collective-permute-start(f32[16,8,2,128]{3,2,1,0:T(2,128)S(1)} %get-tuple-element.29), channel_id=1, source_target_pairs={{0,8},{8,0},{1,9},{9,1},{2,10},{10,2},{3,11},{11,3},{4,12},{12,4},... | collective-permute-start | bytes 393224 | tf_op jit(solution)/shard_map/ppermute | solution.py:32
  42.0 12.0 %all-to-all-start.2 = ((f32[16,3,2,128]{3,2,1,0:T(2,128)}), f32[16,3,2,128]{3,2,1,0:T(2,128)S(1)}, u32[]{:S(2)}, u32[]{:S(2)}) async-start(f32[16,3,2,128]{3,2,1,0:T(2,128)} %get-tuple-element.32), calls=%async_computation.2 | async-start | bytes 98304 | tf_op jit(solution)/shard_map/all_to_all | solution.py:28
  47.0 7.1 %collective-permute-start.1 = (f32[8,2,128]{2,1,0:T(2,128)S(1)}, f32[8,2,128]{2,1,0:T(2,128)S(1)}, u32[]{:S(2)}, u32[]{:S(2)}) collective-permute-start(f32[8,2,128]{2,1,0:T(2,128)S(1)} %get-tuple-element.33.own_ref), channel_id=1, source_target_pairs={{0,8},{8,0},{1,9},{9,1},{2,10},{10,2},{3,11},{11,3},{4,12},{12,4},... | collective-permute-start | bytes 24584 | tf_op jit(solution)/shard_map/ppermute | solution.py:32
